TPU v7x, 1024 devices: a whole 4x8x16 slice. The times are simulated.
1024 devices in a mesh: gx: 4 (over y_hi, core), gy: 16 (over z), gz: 16 (over y_lo, x).
Axes of the slice: x: 4, y: 8 (y_hi: 2, y_lo: 4; y = y_hi * 4 + y_lo), z: 16, core: 2. Of those that a mesh axis runs over, the one named last changes fastest.
Arguments:
- source: float32 [32, 256, 2048], P('gx', 'gy', 'gz'), may hold values from -18 to 18
- pressure_old: float32 [32, 256, 2048], P('gx', 'gy', 'gz'), may hold values from -6 to 6
- strain_prev: float32 [32, 256, 2048], P('gx', 'gy', 'gz'), may hold values from -6 to 6
- motion_old: float32 [3, 32, 256, 2048], P(None, 'gx', 'gy', 'gz'), may hold values from -6 to 6
- body_force: float32 [3, 32, 256, 2048], P(None, 'gx', 'gy', 'gz'), may hold values from -6 to 6
- zone_ids: int32 [32, 256, 2048], P('gx', 'gy', 'gz'), may hold values from 0 to 7
- drained: int32 [32, 256, 2048], P('gx', 'gy', 'gz'), may hold values 0 or 1
- perm_table: float32 [8], replicated, may hold values from 0.1 to 3
- lame_table: float32 [8], replicated, may hold values from 0.5 to 4
- shear_table: float32 [8], replicated, may hold values from 0.3 to 2
Outputs:
- pressure: float32 [32, 256, 2048], P('gx', 'gy', 'gz')
- motion: float32 [3, 32, 256, 2048], P(None, 'gx', 'gy', 'gz')
- strain: float32 [32, 256, 2048], P('gx', 'gy', 'gz')
All inputs are finite; a program needn't handle non-finite values. No bound on the sum of `drained` on one device may be relied on, other than what follows from the above.
Results may differ from a plain program's by a relative error of at most 0.0001.
Values sent between devices are 32-bit elements; how exact they have to be, the bound alone decides.
A program may use at most 32 MiB of HBM per device.

v0:
```python
import functools

import jax
import jax.numpy as jnp
from jax import lax
from jax.sharding import Mesh
from jax.sharding import PartitionSpec as P

ITERS = 2
ZONES = 8
GX_GY_GZ = ("gx_0", "gx_1", "gy", "gz_0", "gz_1")
GX = ("gx_0", "gx_1")
GZ = ("gz_0", "gz_1")


storage = 0.2
biot_coef = 0.8
time_step = 1.0
leakage = 2.0
support = 1.0


def with_halo(shard, sides, width):
    edges = {}
    for axis, dim in sides:
        peers, length = (lax.axis_size(axis), shard.shape[dim])
        up = [(i, (i + 1) % peers) for i in range(peers - 1)]
        last = lax.slice_in_dim(shard, length - width, length, axis=dim)
        initial = lax.slice_in_dim(shard, 0, width, axis=dim)
        edges[dim] = (
            lax.ppermute(last, axis, up),
            lax.ppermute(initial, axis, [(b, a) for a, b in up]),
        )
    done = []
    for _, dim in sides:
        low, high = edges[dim]
        around = [(width, width) if d in done else (0, 0) for d in range(shard.ndim)]
        shard = jnp.concatenate([jnp.pad(low, around), shard, jnp.pad(high, around)], axis=dim)
        done.append(dim)
    return shard


def extended(shard, sides, width):
    for axis, dim in sides:
        peers, length = (lax.axis_size(axis), shard.shape[dim])
        up = [(i, (i + 1) % peers) for i in range(peers - 1)]
        down = [(j, i) for i, j in up]
        last = lax.slice_in_dim(shard, length - width, length, axis=dim)
        initial = lax.slice_in_dim(shard, 0, width, axis=dim)
        before = lax.ppermute(last, axis, up)
        after = lax.ppermute(initial, axis, down)
        shard = jnp.concatenate([before, shard, after], axis=dim)
    return shard


def by_axis(shard, axes):
    return functools.reduce(lax.psum, axes, shard)


def lookup(zone_ids, lookup_table):
    result = jnp.zeros(zone_ids.shape, jnp.float32)
    for zone_index in range(ZONES):
        result = result + jnp.where(zone_ids == zone_index, lookup_table[zone_index], 0.0)
    return result


def interior(padded):
    return padded[..., 1:-1, 1:-1, 1:-1]


def neighbours(padded):
    return [
        padded[..., 2:, 1:-1, 1:-1],
        padded[..., :-2, 1:-1, 1:-1],
        padded[..., 1:-1, 2:, 1:-1],
        padded[..., 1:-1, :-2, 1:-1],
        padded[..., 1:-1, 1:-1, 2:],
        padded[..., 1:-1, 1:-1, :-2],
    ]


def harmonic(own_value, beside):
    return 2.0 * own_value * beside / (own_value + beside)


def central_div(motion_pad):
    return 0.5 * (
        motion_pad[0, 2:, 1:-1, 1:-1]
        - motion_pad[0, :-2, 1:-1, 1:-1]
        + (motion_pad[1, 1:-1, 2:, 1:-1] - motion_pad[1, 1:-1, :-2, 1:-1])
        + (motion_pad[2, 1:-1, 1:-1, 2:] - motion_pad[2, 1:-1, 1:-1, :-2])
    )


def central_grad(press_pad):
    sided = neighbours(press_pad)
    return jnp.stack(
        [0.5 * (sided[0] - sided[1]), 0.5 * (sided[2] - sided[3]), 0.5 * (sided[4] - sided[5])]
    )


def pressure_faces(values):
    return with_halo(values, ((GX, 0), ("gy", 1), (GZ, 2)), 1)


def motion_faces(values):
    return extended(values, ((GX, 1), ("gy", 2), (GZ, 3)), 1)


def products(residual, precond, image):
    return (
        by_axis(jnp.sum(residual * precond), GX_GY_GZ),
        by_axis(jnp.sum(precond * image), GX_GY_GZ),
    )


def conjugate(start_pad, rhs, diag, apply_padded, faces):
    iterate = interior(start_pad)
    tracked = start_pad
    residual = rhs - apply_padded(start_pad)
    precond = residual / diag
    precond_pad = faces(precond)
    image = apply_padded(precond_pad)
    gamma_now, curvature = products(residual, precond, image)
    step_len = gamma_now / curvature
    direction = precond
    direction_pad = precond_pad
    along = image
    for iteration in range(ITERS):
        iterate = iterate + step_len * direction
        residual = residual - step_len * along
        tracked = tracked + step_len * direction_pad
        if iteration + 1 < ITERS:
            precond = residual / diag
            precond_pad = faces(precond)
            image = apply_padded(precond_pad)
            gamma_new, curvature = products(residual, precond, image)
            momentum = gamma_new / gamma_now
            step_len = gamma_new / (curvature - momentum * gamma_new / step_len)
            direction = precond + momentum * direction
            along = image + momentum * along
            direction_pad = precond_pad + momentum * direction_pad
            gamma_now = gamma_new
    return (iterate, tracked)


def shards(
    source,
    pressure_old,
    strain_prev,
    motion_old,
    body_force,
    zone_ids,
    drained,
    perm_table,
    lame_table,
    shear_table,
):
    permeability = lookup(zone_ids, perm_table)
    lame_first = lookup(zone_ids, lame_table)
    shear_mod = lookup(zone_ids, shear_table)
    fixed_term = biot_coef * biot_coef / (lame_first + 2.0 * shear_mod / 3.0)
    stacked = jnp.concatenate(
        [jnp.stack([permeability, lame_first + shear_mod, shear_mod, pressure_old]), motion_old], 0
    )
    padded = extended(stacked, ((GX, 1), ("gy", 2), (GZ, 3)), 1)
    perm_pad = padded[0]
    heft_pad = padded[1]
    shear_pad = padded[2]
    press_pad = padded[3]
    motion_pad = padded[4:7]
    transmit = [harmonic(permeability, beside) for beside in neighbours(perm_pad)]
    reaction = storage + fixed_term + leakage * drained.astype(jnp.float32)
    pdiag = reaction + time_step * sum(transmit)

    def apply_pressure(field_pad):
        center = interior(field_pad)
        flux = sum(
            (factor * (center - beside) for factor, beside in zip(transmit, neighbours(field_pad)))
        )
        return reaction * center + time_step * flux

    prhs = (
        source
        + (storage + fixed_term) * pressure_old
        - biot_coef * (central_div(motion_pad) - strain_prev)
    )
    pressure, pressure_kept = conjugate(press_pad, prhs, pdiag, apply_pressure, pressure_faces)
    heft = interior(heft_pad)
    shear_faces = [harmonic(shear_mod, beside) for beside in neighbours(shear_pad)]
    heft_sides = neighbours(heft_pad)
    base_diag = support + sum(shear_faces) + heft
    ediag = jnp.stack(
        [base_diag + heft_sides[1], base_diag + heft_sides[3], base_diag + heft_sides[5]]
    )

    def apply_motion(field_pad):
        center = interior(field_pad)
        spread = sum(
            (
                factor * (center - beside)
                for factor, beside in zip(shear_faces, neighbours(field_pad))
            )
        )
        diverg = (
            field_pad[0, 1:, :-1, :-1]
            - field_pad[0, :-1, :-1, :-1]
            + (field_pad[1, :-1, 1:, :-1] - field_pad[1, :-1, :-1, :-1])
            + (field_pad[2, :-1, :-1, 1:] - field_pad[2, :-1, :-1, :-1])
        )
        scaled = heft_pad[:-1, :-1, :-1] * diverg
        own_part = scaled[1:, 1:, 1:]
        push = jnp.stack(
            [
                scaled[:-1, 1:, 1:] - own_part,
                scaled[1:, :-1, 1:] - own_part,
                scaled[1:, 1:, :-1] - own_part,
            ]
        )
        return support * center + spread + push

    erhs = body_force - biot_coef * central_grad(pressure_kept)
    motion, motion_kept = conjugate(motion_pad, erhs, ediag, apply_motion, motion_faces)
    strain = central_div(motion_kept)
    return (pressure, motion, strain)


def solution(mesh):
    torus = Mesh(
        mesh.devices.reshape(2, 2, mesh.shape["gy"], 4, 4), ("gx_0", "gx_1", "gy", "gz_0", "gz_1")
    )
    return jax.shard_map(
        shards,
        mesh=torus,
        in_specs=(
            P(GX, "gy", GZ),
            P(GX, "gy", GZ),
            P(GX, "gy", GZ),
            P(None, GX, "gy", GZ),
            P(None, GX, "gy", GZ),
            P(GX, "gy", GZ),
            P(GX, "gy", GZ),
            P(),
            P(),
            P(),
        ),
        out_specs=(P(GX, "gy", GZ), P(None, GX, "gy", GZ), P(GX, "gy", GZ)),
        check_vma=False,
    )
```

profile of v0, /device:TPU:8, one launch (start us, length us, event | category | flops | bytes accessed | tf_op | source)
XLA Modules:
  0.0 479.0 jit_solution(2596816173895060521)
XLA Ops:
  3.6 6.6 %bitcast_dynamic-update-slice_fusion.3 = (f32[7,8,16,128]{3,2,1,0:T(8,128)S(1)}, f32[8,16,128]{2,1,0:T(8,128)}, pred[8,16,128]{2,1,0:T(8,128)(4,1)S(1)}, pred[8,...) fusion(f32[]{:T(128)} %bitcast.7, f32[]{:T(128)} %bitcast.6, ...), kind=kLoop, calls=%fused_computation.306 | loop fusion | flops 376831 | bytes 327712
  10.3 10.7 %bitcast_dynamic-update-slice_fusion.2 = (f32[7,8,16,128]{3,2,1,0:T(8,128)S(1)}, f32[8,16,128]{2,1,0:T(8,128)S(1)}, f32[8,16,128]{2,1,0:T(8,128)}) fusion(f32[7,8,16,128]{3,2,1,0:T(8,128)S(1)} %get-tuple-element.89, pred[8,16,128]{2,1,0:T(8,128)(4,1)S(1)} %get-tuple-element.98, f32[]{:T(128)} %bitcast.24, pred[8,16,128]{2,1,0:T(8,128)(4,1)S(1)} %get-tuple-element.97, ...), kind=kLoop, calls=%fused_computation.305 | loop fusion | flops 507904 | bytes 327744
  25.0 6.5 %collective-permute-done.1 = f32[7,1,16,128]{3,2,1,0:T(8,128)S(1)} collective-permute-done((f32[7,1,16,128]{3,2,1,0:T(8,128)S(1)}, f32[7,1,16,128]{3,2,1,0:T(8,128)S(1)}, u32[]{:S(2)}, u32[]{:S(2)}) %collective-permute-start.1) | collective-permute-done | bytes 57376 | tf_op jit(solution)/shard_map/ppermute | solution.py:51
  55.8 6.3 %collective-permute-start.10 = (f32[8,16,1]{2,1,0:T(8,128)S(1)}, f32[8,16,1]{2,1,0:T(8,128)S(1)}, u32[]{:S(2)}, u32[]{:S(2)}) collective-permute-start(f32[8,16,1]{2,1,0:T(8,128)S(1)} %get-tuple-element.143), channel_id=1, source_target_pairs={{1,0},{2,1},{3,2},{4,3},{5,4},{6,5},{7,6},{8,7},{9,8},{10,9},{11,1... | collective-permute-start | bytes 1544 | tf_op jit(solution)/shard_map/ppermute | solution.py:32
  70.2 6.1 %collective-permute-start.7 = (f32[1,16,128]{2,1,0:T(8,128)S(1)}, f32[1,16,128]{2,1,0:T(8,128)S(1)}, u32[]{:S(2)}, u32[]{:S(2)}) collective-permute-start(f32[1,16,128]{2,1,0:T(8,128)S(1)} %get-tuple-element.147), channel_id=1, source_target_pairs={{0,256},{256,512},{512,768},{1,257},{257,513},{513,769},{2,258},{2... | collective-permute-start | bytes 24584 | tf_op jit(solution)/shard_map/ppermute | solution.py:31
  87.6 12.7 %all-reduce.27 = (f32[]{:T(128)}, f32[]{:T(128)}) all-reduce(f32[]{:T(128)} %get-tuple-element.21, f32[]{:T(128)} %get-tuple-element.20), channel_id=1, replica_groups=mesh['gx_0'=2,'gx_1'=2,'gy'=16,'gz_0'=4,'gz_1'=4] {'gx_0'}, use_global_device_ids=true, to_apply=%region_1.2 | all-reduce | flops 2 | bytes 16 | tf_op jit(solution)/shard_map/psum | solution.py:57
  103.4 41.7 %all-reduce.11 = (f32[]{:T(128)}, f32[]{:T(128)}) all-reduce(f32[]{:T(128)} %get-tuple-element.52, f32[]{:T(128)} %get-tuple-element.53), channel_id=1, replica_groups=mesh['gx_0'=2,'gx_1'=2,'gy'=16,'gz_0'=4,'gz_1'=4] {'gy'}, use_global_device_ids=true, to_apply=%region_3.4 | all-reduce | flops 2 | bytes 16 | tf_op jit(solution)/shard_map/psum | solution.py:57
  145.1 8.1 %all-reduce.19 = (f32[]{:T(128)}, f32[]{:T(128)}) all-reduce(f32[]{:T(128)} %get-tuple-element.28, f32[]{:T(128)} %get-tuple-element.29), channel_id=1, replica_groups=mesh['gx_0'=2,'gx_1'=2,'gy'=16,'gz_0'=4,'gz_1'=4] {'gz_0'}, use_global_device_ids=true, to_apply=%region_4.5 | all-reduce | flops 2 | bytes 16 | tf_op jit(solution)/shard_map/psum | solution.py:57
  153.1 9.5 %all-reduce.15 = (f32[]{:T(128)}, f32[]{:T(128)}) all-reduce(f32[]{:T(128)} %get-tuple-element.44, f32[]{:T(128)} %get-tuple-element.45), channel_id=1, replica_groups=mesh['gx_0'=2,'gx_1'=2,'gy'=16,'gz_0'=4,'gz_1'=4] {'gz_1'}, use_global_device_ids=true, to_apply=%region_5.6 | all-reduce | flops 2 | bytes 16 | tf_op jit(solution)/shard_map/psum | solution.py:57
  186.8 16.3 %all-reduce.26 = (f32[]{:T(128)}, f32[]{:T(128)}) all-reduce(f32[]{:T(128)} %get-tuple-element.136, f32[]{:T(128)} %fusion.102), channel_id=1, replica_groups=mesh['gx_0'=2,'gx_1'=2,'gy'=16,'gz_0'=4,'gz_1'=4] {'gx_0'}, use_global_device_ids=true, to_apply=%region_13.14 | all-reduce | flops 2 | bytes 16 | tf_op jit(solution)/shard_map/psum | solution.py:57
  206.3 30.6 %all-reduce.10 = (f32[]{:T(128)}, f32[]{:T(128)}) all-reduce(f32[]{:T(128)} %get-tuple-element.50, f32[]{:T(128)} %get-tuple-element.51), channel_id=1, replica_groups=mesh['gx_0'=2,'gx_1'=2,'gy'=16,'gz_0'=4,'gz_1'=4] {'gy'}, use_global_device_ids=true, to_apply=%region_15.16 | all-reduce | flops 2 | bytes 16 | tf_op jit(solution)/shard_map/psum | solution.py:57
  236.9 7.2 %all-reduce.18 = (f32[]{:T(128)}, f32[]{:T(128)}) all-reduce(f32[]{:T(128)} %get-tuple-element.26, f32[]{:T(128)} %get-tuple-element.27), channel_id=1, replica_groups=mesh['gx_0'=2,'gx_1'=2,'gy'=16,'gz_0'=4,'gz_1'=4] {'gz_0'}, use_global_device_ids=true, to_apply=%region_16.17 | all-reduce | flops 2 | bytes 16 | tf_op jit(solution)/shard_map/psum | solution.py:57
  244.1 10.4 %all-reduce.14 = (f32[]{:T(128)}, f32[]{:T(128)}) all-reduce(f32[]{:T(128)} %get-tuple-element.42, f32[]{:T(128)} %get-tuple-element.43), channel_id=1, replica_groups=mesh['gx_0'=2,'gx_1'=2,'gy'=16,'gz_0'=4,'gz_1'=4] {'gz_1'}, use_global_device_ids=true, to_apply=%region_17.18 | all-reduce | flops 2 | bytes 16 | tf_op jit(solution)/shard_map/psum | solution.py:57
  264.6 7.9 %collective-permute-done.18 = f32[3,1,16,128]{3,2,1,0:T(8,128)S(1)} collective-permute-done((f32[3,1,16,128]{3,2,1,0:T(8,128)S(1)}, f32[3,1,16,128]{3,2,1,0:T(8,128)S(1)}, u32[]{:S(2)}, u32[]{:S(2)}) %collective-permute-start.18) | collective-permute-done | bytes 24608 | tf_op jit(solution)/shard_map/ppermute | solution.py:51
  284.1 6.0 %collective-permute-start.22 = (f32[3,10,18,1]{3,2,1,0:T(8,128)S(1)}, f32[3,10,18,1]{3,2,1,0:T(8,128)S(1)}, u32[]{:S(2)}, u32[]{:S(2)}) collective-permute-start(f32[3,10,18,1]{3,2,1,0:T(8,128)S(1)} %get-tuple-element.111), channel_id=1, source_target_pairs={{1,0},{2,1},{3,2},{4,3},{5,4},{6,5},{7,6},{8,7},{9,8},{10,9},{11,1... | collective-permute-start | bytes 6488 | tf_op jit(solution)/shard_map/ppermute | solution.py:51
  296.8 9.9 %all-reduce.25 = (f32[]{:T(128)}, f32[]{:T(128)}) all-reduce(f32[]{:T(128)} %get-tuple-element.19, f32[]{:T(128)} %get-tuple-element.18), channel_id=1, replica_groups=mesh['gx_0'=2,'gx_1'=2,'gy'=16,'gz_0'=4,'gz_1'=4] {'gx_0'}, use_global_device_ids=true, to_apply=%region_25.26 | all-reduce | flops 2 | bytes 16 | tf_op jit(solution)/shard_map/psum | solution.py:57
  312.1 30.1 %all-reduce.9 = (f32[]{:T(128)}, f32[]{:T(128)}) all-reduce(f32[]{:T(128)} %get-tuple-element.48, f32[]{:T(128)} %get-tuple-element.49), channel_id=1, replica_groups=mesh['gx_0'=2,'gx_1'=2,'gy'=16,'gz_0'=4,'gz_1'=4] {'gy'}, use_global_device_ids=true, to_apply=%region_27.28 | all-reduce | flops 2 | bytes 16 | tf_op jit(solution)/shard_map/psum | solution.py:57
  342.2 10.9 %all-reduce.17 = (f32[]{:T(128)}, f32[]{:T(128)}) all-reduce(f32[]{:T(128)} %get-tuple-element.24, f32[]{:T(128)} %get-tuple-element.25), channel_id=1, replica_groups=mesh['gx_0'=2,'gx_1'=2,'gy'=16,'gz_0'=4,'gz_1'=4] {'gz_0'}, use_global_device_ids=true, to_apply=%region_28.29 | all-reduce | flops 2 | bytes 16 | tf_op jit(solution)/shard_map/psum | solution.py:57
  353.1 11.4 %all-reduce.13 = (f32[]{:T(128)}, f32[]{:T(128)}) all-reduce(f32[]{:T(128)} %get-tuple-element.40, f32[]{:T(128)} %get-tuple-element.41), channel_id=1, replica_groups=mesh['gx_0'=2,'gx_1'=2,'gy'=16,'gz_0'=4,'gz_1'=4] {'gz_1'}, use_global_device_ids=true, to_apply=%region_29.30 | all-reduce | flops 2 | bytes 16 | tf_op jit(solution)/shard_map/psum | solution.py:57
  386.3 6.2 %collective-permute-start.28 = (f32[3,10,18,1]{3,2,1,0:T(8,128)S(1)}, f32[3,10,18,1]{3,2,1,0:T(8,128)S(1)}, u32[]{:S(2)}, u32[]{:S(2)}) collective-permute-start(f32[3,10,18,1]{3,2,1,0:T(8,128)S(1)} %get-tuple-element.109), channel_id=1, source_target_pairs={{1,0},{2,1},{3,2},{4,3},{5,4},{6,5},{7,6},{8,7},{9,8},{10,9},{11,1... | collective-permute-start | bytes 6488 | tf_op jit(solution)/shard_map/ppermute | solution.py:51
  399.3 9.9 %all-reduce.24 = (f32[]{:T(128)}, f32[]{:T(128)}) all-reduce(f32[]{:T(128)} %get-tuple-element.62, f32[]{:T(128)} %fusion.23), channel_id=1, replica_groups=mesh['gx_0'=2,'gx_1'=2,'gy'=16,'gz_0'=4,'gz_1'=4] {'gx_0'}, use_global_device_ids=true, to_apply=%region_37.38 | all-reduce | flops 2 | bytes 16 | tf_op jit(solution)/shard_map/psum | solution.py:57
  414.5 32.4 %all-reduce.8 = (f32[]{:T(128)}, f32[]{:T(128)}) all-reduce(f32[]{:T(128)} %get-tuple-element.46, f32[]{:T(128)} %get-tuple-element.47), channel_id=1, replica_groups=mesh['gx_0'=2,'gx_1'=2,'gy'=16,'gz_0'=4,'gz_1'=4] {'gy'}, use_global_device_ids=true, to_apply=%region_39.40 | all-reduce | flops 2 | bytes 16 | tf_op jit(solution)/shard_map/psum | solution.py:57
  447.0 7.1 %all-reduce.16 = (f32[]{:T(128)}, f32[]{:T(128)}) all-reduce(f32[]{:T(128)} %get-tuple-element.22, f32[]{:T(128)} %get-tuple-element.23), channel_id=1, replica_groups=mesh['gx_0'=2,'gx_1'=2,'gy'=16,'gz_0'=4,'gz_1'=4] {'gz_0'}, use_global_device_ids=true, to_apply=%region_40.41 | all-reduce | flops 2 | bytes 16 | tf_op jit(solution)/shard_map/psum | solution.py:57
  454.1 15.0 %all-reduce.12 = (f32[]{:T(128)}, f32[]{:T(128)}) all-reduce(f32[]{:T(128)} %get-tuple-element.38, f32[]{:T(128)} %get-tuple-element.39), channel_id=1, replica_groups=mesh['gx_0'=2,'gx_1'=2,'gy'=16,'gz_0'=4,'gz_1'=4] {'gz_1'}, use_global_device_ids=true, to_apply=%region_41.42 | all-reduce | flops 2 | bytes 16 | tf_op jit(solution)/shard_map/psum | solution.py:57
  (286 shorter events, 145.5 us)
Async XLA Ops:
  23.7 7.8 %collective-permute-start.1 = (f32[7,1,16,128]{3,2,1,0:T(8,128)S(1)}, f32[7,1,16,128]{3,2,1,0:T(8,128)S(1)}, u32[]{:S(2)}, u32[]{:S(2)}) collective-permute-start(f32[7,1,16,128]{3,2,1,0:T(8,128)S(1)} %get-tuple-element.108), channel_id=1, source_target_pairs={{256,0},{512,256},{768,512},{257,1},{513,257},{769,513},{258,2},{5... | collective-permute-start | bytes 172040 | tf_op jit(solution)/shard_map/ppermute | solution.py:51
  31.6 5.9 %collective-permute-start.2 = (f32[7,10,1,128]{3,2,1,0:T(1,128)S(1)}, f32[7,10,1,128]{3,2,1,0:T(1,128)S(1)}, u32[]{:S(2)}, u32[]{:S(2)}) collective-permute-start(f32[7,10,1,128]{3,2,1,0:T(1,128)S(1)} %get-tuple-element.105), channel_id=1, source_target_pairs={{0,16},{16,32},{32,48},{48,64},{64,80},{80,96},{96,112},{112,128},... | collective-permute-start | bytes 107528 | tf_op jit(solution)/shard_map/ppermute | solution.py:50
  35.8 6.2 %collective-permute-start.3 = (f32[7,10,1,128]{3,2,1,0:T(1,128)S(1)}, f32[7,10,1,128]{3,2,1,0:T(1,128)S(1)}, u32[]{:S(2)}, u32[]{:S(2)}) collective-permute-start(f32[7,10,1,128]{3,2,1,0:T(1,128)S(1)} %get-tuple-element.106), channel_id=1, source_target_pairs={{16,0},{32,16},{48,32},{64,48},{80,64},{96,80},{112,96},{128,112},... | collective-permute-start | bytes 107528 | tf_op jit(solution)/shard_map/ppermute | solution.py:51
  43.0 8.5 %collective-permute-start.4 = (f32[7,10,18,1]{2,3,1,0:T(1,128)S(1)}, f32[7,10,18,1]{2,3,1,0:T(1,128)S(1)}, u32[]{:S(2)}, u32[]{:S(2)}) collective-permute-start(f32[7,10,18,1]{2,3,1,0:T(1,128)S(1)} %copy.606), channel_id=1, source_target_pairs={{0,1},{1,2},{2,3},{3,4},{4,5},{5,6},{6,7},{7,8},{8,9},{9,10},{10,1... | collective-permute-start | bytes 15128 | tf_op jit(solution)/shard_map/ppermute | solution.py:50
  46.9 6.2 %collective-permute-start.5 = (f32[7,10,18,1]{2,3,1,0:T(1,128)S(1)}, f32[7,10,18,1]{2,3,1,0:T(1,128)S(1)}, u32[]{:S(2)}, u32[]{:S(2)}) collective-permute-start(f32[7,10,18,1]{2,3,1,0:T(1,128)S(1)} %copy.607), channel_id=1, source_target_pairs={{1,0},{2,1},{3,2},{4,3},{5,4},{6,5},{7,6},{8,7},{9,8},{10,9},{11,1... | collective-permute-start | bytes 15128 | tf_op jit(solution)/shard_map/ppermute | solution.py:51
  55.8 21.9 %collective-permute-start.10 = (f32[8,16,1]{2,1,0:T(8,128)S(1)}, f32[8,16,1]{2,1,0:T(8,128)S(1)}, u32[]{:S(2)}, u32[]{:S(2)}) collective-permute-start(f32[8,16,1]{2,1,0:T(8,128)S(1)} %get-tuple-element.143), channel_id=1, source_target_pairs={{1,0},{2,1},{3,2},{4,3},{5,4},{6,5},{7,6},{8,7},{9,8},{10,9},{11,1... | collective-permute-start | bytes 1544 | tf_op jit(solution)/shard_map/ppermute | solution.py:32
  64.6 21.4 %collective-permute-start.9 = (f32[8,1,128]{2,1,0:T(1,128)S(1)}, f32[8,1,128]{2,1,0:T(1,128)S(1)}, u32[]{:S(2)}, u32[]{:S(2)}) collective-permute-start(f32[8,1,128]{2,1,0:T(1,128)S(1)} %get-tuple-element.145), channel_id=1, source_target_pairs={{0,16},{16,32},{32,48},{48,64},{64,80},{80,96},{96,112},{112,128},... | collective-permute-start | bytes 12296 | tf_op jit(solution)/shard_map/ppermute | solution.py:31
  68.9 17.2 %collective-permute-start.8 = (f32[8,1,128]{2,1,0:T(1,128)S(1)}, f32[8,1,128]{2,1,0:T(1,128)S(1)}, u32[]{:S(2)}, u32[]{:S(2)}) collective-permute-start(f32[8,1,128]{2,1,0:T(1,128)S(1)} %get-tuple-element.146), channel_id=1, source_target_pairs={{16,0},{32,16},{48,32},{64,48},{80,64},{96,80},{112,96},{128,112},... | collective-permute-start | bytes 12296 | tf_op jit(solution)/shard_map/ppermute | solution.py:32
  70.2 15.9 %collective-permute-start.7 = (f32[1,16,128]{2,1,0:T(8,128)S(1)}, f32[1,16,128]{2,1,0:T(8,128)S(1)}, u32[]{:S(2)}, u32[]{:S(2)}) collective-permute-start(f32[1,16,128]{2,1,0:T(8,128)S(1)} %get-tuple-element.147), channel_id=1, source_target_pairs={{0,256},{256,512},{512,768},{1,257},{257,513},{513,769},{2,258},{2... | collective-permute-start | bytes 24584 | tf_op jit(solution)/shard_map/ppermute | solution.py:31
  76.3 9.8 %collective-permute-start.6 = (f32[1,16,128]{2,1,0:T(8,128)S(1)}, f32[1,16,128]{2,1,0:T(8,128)S(1)}, u32[]{:S(2)}, u32[]{:S(2)}) collective-permute-start(f32[1,16,128]{2,1,0:T(8,128)S(1)} %get-tuple-element.148), channel_id=1, source_target_pairs={{256,0},{512,256},{768,512},{257,1},{513,257},{769,513},{258,2},{5... | collective-permute-start | bytes 24584 | tf_op jit(solution)/shard_map/ppermute | solution.py:32
  77.7 8.4 %collective-permute-start.11 = (f32[8,16,1]{2,1,0:T(8,128)S(1)}, f32[8,16,1]{2,1,0:T(8,128)S(1)}, u32[]{:S(2)}, u32[]{:S(2)}) collective-permute-start(f32[8,16,1]{2,1,0:T(8,128)S(1)} %get-tuple-element.144), channel_id=1, source_target_pairs={{0,1},{1,2},{2,3},{3,4},{4,5},{5,6},{6,7},{7,8},{8,9},{9,10},{10,1... | collective-permute-start | bytes 1544 | tf_op jit(solution)/shard_map/ppermute | solution.py:31
  165.6 12.0 %collective-permute-start.16 = (f32[8,16,1]{2,1,0:T(8,128)S(1)}, f32[8,16,1]{2,1,0:T(8,128)S(1)}, u32[]{:S(2)}, u32[]{:S(2)}) collective-permute-start(f32[8,16,1]{2,1,0:T(8,128)S(1)} %get-tuple-element.137), channel_id=1, source_target_pairs={{1,0},{2,1},{3,2},{4,3},{5,4},{6,5},{7,6},{8,7},{9,8},{10,9},{11,1... | collective-permute-start | bytes 1544 | tf_op jit(solution)/shard_map/ppermute | solution.py:32
  170.9 14.9 %collective-permute-start.15 = (f32[8,1,128]{2,1,0:T(1,128)S(1)}, f32[8,1,128]{2,1,0:T(1,128)S(1)}, u32[]{:S(2)}, u32[]{:S(2)}) collective-permute-start(f32[8,1,128]{2,1,0:T(1,128)S(1)} %get-tuple-element.141), channel_id=1, source_target_pairs={{0,16},{16,32},{32,48},{48,64},{64,80},{80,96},{96,112},{112,128},... | collective-permute-start | bytes 12296 | tf_op jit(solution)/shard_map/ppermute | solution.py:31
  173.6 12.2 %collective-permute-start.14 = (f32[8,1,128]{2,1,0:T(1,128)S(1)}, f32[8,1,128]{2,1,0:T(1,128)S(1)}, u32[]{:S(2)}, u32[]{:S(2)}) collective-permute-start(f32[8,1,128]{2,1,0:T(1,128)S(1)} %get-tuple-element.142), channel_id=1, source_target_pairs={{16,0},{32,16},{48,32},{64,48},{80,64},{96,80},{112,96},{128,112},... | collective-permute-start | bytes 12296 | tf_op jit(solution)/shard_map/ppermute | solution.py:32
  174.9 11.0 %collective-permute-start.13 = (f32[1,16,128]{2,1,0:T(8,128)S(1)}, f32[1,16,128]{2,1,0:T(8,128)S(1)}, u32[]{:S(2)}, u32[]{:S(2)}) collective-permute-start(f32[1,16,128]{2,1,0:T(8,128)S(1)} %get-tuple-element.139), channel_id=1, source_target_pairs={{0,256},{256,512},{512,768},{1,257},{257,513},{513,769},{2,258},{2... | collective-permute-start | bytes 24584 | tf_op jit(solution)/shard_map/ppermute | solution.py:31
  176.2 9.7 %collective-permute-start.12 = (f32[1,16,128]{2,1,0:T(8,128)S(1)}, f32[1,16,128]{2,1,0:T(8,128)S(1)}, u32[]{:S(2)}, u32[]{:S(2)}) collective-permute-start(f32[1,16,128]{2,1,0:T(8,128)S(1)} %get-tuple-element.140), channel_id=1, source_target_pairs={{256,0},{512,256},{768,512},{257,1},{513,257},{769,513},{258,2},{5... | collective-permute-start | bytes 24584 | tf_op jit(solution)/shard_map/ppermute | solution.py:32
  177.6 8.3 %collective-permute-start.17 = (f32[8,16,1]{2,1,0:T(8,128)S(1)}, f32[8,16,1]{2,1,0:T(8,128)S(1)}, u32[]{:S(2)}, u32[]{:S(2)}) collective-permute-start(f32[8,16,1]{2,1,0:T(8,128)S(1)} %get-tuple-element.138), channel_id=1, source_target_pairs={{0,1},{1,2},{2,3},{3,4},{4,5},{5,6},{6,7},{7,8},{8,9},{9,10},{10,1... | collective-permute-start | bytes 1544 | tf_op jit(solution)/shard_map/ppermute | solution.py:31
  263.3 9.3 %collective-permute-start.18 = (f32[3,1,16,128]{3,2,1,0:T(8,128)S(1)}, f32[3,1,16,128]{3,2,1,0:T(8,128)S(1)}, u32[]{:S(2)}, u32[]{:S(2)}) collective-permute-start(f32[3,1,16,128]{3,2,1,0:T(8,128)S(1)} %get-tuple-element.134), channel_id=1, source_target_pairs={{256,0},{512,256},{768,512},{257,1},{513,257},{769,513},{258,2},{5... | collective-permute-start | bytes 73736 | tf_op jit(solution)/shard_map/ppermute | solution.py:51
  276.3 5.6 %collective-permute-start.20 = (f32[3,10,1,128]{3,2,1,0:T(1,128)S(1)}, f32[3,10,1,128]{3,2,1,0:T(1,128)S(1)}, u32[]{:S(2)}, u32[]{:S(2)}) collective-permute-start(f32[3,10,1,128]{3,2,1,0:T(1,128)S(1)} %get-tuple-element.118), channel_id=1, source_target_pairs={{16,0},{32,16},{48,32},{64,48},{80,64},{96,80},{112,96},{128,112},... | collective-permute-start | bytes 46088 | tf_op jit(solution)/shard_map/ppermute | solution.py:51
  282.1 11.5 %collective-permute-start.23 = (f32[3,10,18,1]{3,2,1,0:T(8,128)S(1)}, f32[3,10,18,1]{3,2,1,0:T(8,128)S(1)}, u32[]{:S(2)}, u32[]{:S(2)}) collective-permute-start(f32[3,10,18,1]{3,2,1,0:T(8,128)S(1)} %get-tuple-element.112), channel_id=1, source_target_pairs={{0,1},{1,2},{2,3},{3,4},{4,5},{5,6},{6,7},{7,8},{8,9},{9,10},{10,1... | collective-permute-start | bytes 6488 | tf_op jit(solution)/shard_map/ppermute | solution.py:50
  284.1 11.0 %collective-permute-start.22 = (f32[3,10,18,1]{3,2,1,0:T(8,128)S(1)}, f32[3,10,18,1]{3,2,1,0:T(8,128)S(1)}, u32[]{:S(2)}, u32[]{:S(2)}) collective-permute-start(f32[3,10,18,1]{3,2,1,0:T(8,128)S(1)} %get-tuple-element.111), channel_id=1, source_target_pairs={{1,0},{2,1},{3,2},{4,3},{5,4},{6,5},{7,6},{8,7},{9,8},{10,9},{11,1... | collective-permute-start | bytes 6488 | tf_op jit(solution)/shard_map/ppermute | solution.py:51
  368.9 7.3 %collective-permute-start.24 = (f32[3,1,16,128]{3,2,1,0:T(8,128)S(1)}, f32[3,1,16,128]{3,2,1,0:T(8,128)S(1)}, u32[]{:S(2)}, u32[]{:S(2)}) collective-permute-start(f32[3,1,16,128]{3,2,1,0:T(8,128)S(1)} %get-tuple-element.132), channel_id=1, source_target_pairs={{256,0},{512,256},{768,512},{257,1},{513,257},{769,513},{258,2},{5... | collective-permute-start | bytes 73736 | tf_op jit(solution)/shard_map/ppermute | solution.py:51
  383.6 11.5 %collective-permute-start.29 = (f32[3,10,18,1]{3,2,1,0:T(8,128)S(1)}, f32[3,10,18,1]{3,2,1,0:T(8,128)S(1)}, u32[]{:S(2)}, u32[]{:S(2)}) collective-permute-start(f32[3,10,18,1]{3,2,1,0:T(8,128)S(1)} %get-tuple-element.110), channel_id=1, source_target_pairs={{0,1},{1,2},{2,3},{3,4},{4,5},{5,6},{6,7},{7,8},{8,9},{9,10},{10,1... | collective-permute-start | bytes 6488 | tf_op jit(solution)/shard_map/ppermute | solution.py:50
  386.3 11.0 %collective-permute-start.28 = (f32[3,10,18,1]{3,2,1,0:T(8,128)S(1)}, f32[3,10,18,1]{3,2,1,0:T(8,128)S(1)}, u32[]{:S(2)}, u32[]{:S(2)}) collective-permute-start(f32[3,10,18,1]{3,2,1,0:T(8,128)S(1)} %get-tuple-element.109), channel_id=1, source_target_pairs={{1,0},{2,1},{3,2},{4,3},{5,4},{6,5},{7,6},{8,7},{9,8},{10,9},{11,1... | collective-permute-start | bytes 6488 | tf_op jit(solution)/shard_map/ppermute | solution.py:51
  (89 other events, 1280.7 us)
where the time goes:
time: 481 us; the launch traced here: 479 us
  blocking collectives  280 us (58%)
  starting transfers between devices  80.6 us (17%)
  waiting for transfers between devices  53.8 us (11%)
  other arithmetic  39 us (8%)
  between operations  13.9 us (3%)
  local copies, waits for them, and re-layouts  11.4 us (2%)
    psum x20, blocking collectives, by_axis(): return functools.reduce(lax.psum, axes, shard)  280 us
    ppermute x9, waiting for transfers between devices, extended(): after = lax.ppermute(initial, axis, down)  35.9 us
    ppermute x9, starting transfers between devices, extended(): after = lax.ppermute(initial, axis, down)  24.5 us
    ppermute x9, starting transfers between devices, extended(): before = lax.ppermute(last, axis, up)  21 us
    ppermute x6, starting transfers between devices, with_halo(): lax.ppermute(last, axis, up)  18.3 us
    unnamed x2, other arithmetic  17.3 us
    ppermute x6, starting transfers between devices, with_halo(): lax.ppermute(initial, axis, [(b, a) for a, b in up])  16.8 us
    ppermute x6, waiting for transfers between devices, with_halo(): lax.ppermute(last, axis, up)  11.2 us
  transfers between devices with their start and end apart: 30, of which 16 were waited for; matrix products, arithmetic and copies ran while one was open for 1% of the time, Pallas kernels for 0%

commit v1 on v0

v1 whole, which is shorter than its diff:
```python
import functools

import jax
import jax.numpy as jnp
from jax import lax
from jax.experimental import pallas as pl
from jax.experimental.pallas import tpu as pltpu
from jax.sharding import PartitionSpec as P

ZONES = 8
MESH = pl.DeviceIdType.MESH
F32 = jnp.float32
WIN = (4, 24)
OWN = (8, 16)
L, R = (16, 17)


def lanes(rows):
    return lax.broadcasted_iota(jnp.int32, (rows, 128), 1)


class Row:
    def __init__(self, i, window, strip):
        self.i, self.strip = (i, strip)
        self.start, self.count = window
        self.lane = lanes(self.count)

    def at(self, ref, f, dy=0, i=None):
        return ref[f, self.i if i is None else i, pl.ds(self.start + dy, self.count), :]

    def xp(self, ref, f):
        if self.strip:
            return pltpu.roll(self.at(ref, f), 120, 1)
        return self.at(ref, f, i=self.i + 1)

    def xm(self, ref, f):
        if self.strip:
            return pltpu.roll(self.at(ref, f), 8, 1)
        return self.at(ref, f, i=self.i - 1)

    def yp(self, ref, f):
        return self.at(ref, f, dy=1)

    def ym(self, ref, f):
        return self.at(ref, f, dy=-1)

    def zp(self, ref, f):
        turned = pltpu.roll(self.at(ref, f), 127, 1)
        if self.strip:
            return turned
        edge = pltpu.roll(self.at(ref, f, i=R), 123 - 8 * self.i, 1)
        return jnp.where(self.lane == 127, edge, turned)

    def zm(self, ref, f):
        turned = pltpu.roll(self.at(ref, f), 1, 1)
        if self.strip:
            return turned
        edge = pltpu.roll(self.at(ref, f, i=L), 125 - 8 * self.i, 1)
        return jnp.where(self.lane == 0, edge, turned)

    def put(self, ref, f, value):
        ref[f, self.i, pl.ds(self.start, self.count), :] = value


def over_rows(low, high, body, window=WIN, strips=(L, R)):
    @pl.loop(low, high)
    def _(i):
        body(Row(i, window, False))

    if strips:

        @pl.loop(strips[0], strips[-1] + 1)
        def _(i):
            body(Row(i, window, True))


def harmonic(own, beside):
    total = own + beside
    return 2.0 * own * beside / jnp.where(total > 0.0, total, 1.0)


def fold(value):
    return value[0:8] + value[8:16]


def kernel(
    sizes,
    source,
    press_old,
    strain_prev,
    motion_old,
    body_force,
    zones,
    drained,
    perm_t,
    lame_t,
    shear_t,
    press_out,
    motion_out,
    strain_out,
    own_src,
    own_strain,
    own_bf,
    own_zone,
    own_drain,
    zd,
    xu,
    z0,
    ze,
    mat,
    tf,
    mf,
    diag,
    ediag,
    sp,
    gv,
    se,
    mo,
    pk_zd,
    pk_xu,
    pk_z0,
    pk_ze,
    pl_zd,
    pl_xu,
    pl_z0,
    pl_ze,
    pr_zd,
    pr_xu,
    pr_z0,
    pr_ze,
    ys_zd,
    ys_xu,
    ys_z0,
    ys_ze,
    yr_zd,
    yr_xu,
    yr_z0,
    yr_ze,
    rows,
    part,
    got_a,
    got_b,
    got_c,
    load_sem,
    xs_sem,
    xr_sem,
    zs_sem,
    zr_sem,
    yss_sem,
    yrs_sem,
    rs_sem,
    rr_sem,
    known,
):
    nx, ny, nz, cores, xs = sizes
    gx, gy, gz = (lax.axis_index("gx"), lax.axis_index("gy"), lax.axis_index("gz"))
    yhs, yls = (nx // cores, nz // xs)
    x_lo, x_hi = (gx > 0, gx < nx - 1)
    y_lo, y_hi = (gy > 0, gy < ny - 1)
    z_lo, z_hi = (gz > 0, gz < nz - 1)

    def turn(value, by, count):
        return lax.rem(value + (by % count), count)

    beside = []
    for by in (1, -1):
        if nx > 1:
            beside.append((turn(gx, by, nx), gy, gz))
        if ny > 1:
            beside.append((gx, turn(gy, by, ny), gz))
        if nz > 1:
            beside.append((gx, gy, turn(gz, by, nz)))
    yh, core = (gx // cores, lax.rem(gx, cores))
    yl, xx = (gz // xs, lax.rem(gz, xs))
    group_a = [
        (yh * cores + turn(core, c, cores), gy, yl * xs + turn(xx, x, xs))
        for c in range(cores)
        for x in range(xs)
        if c or x
    ]
    group_b = [
        (turn(yh, h, yhs) * cores + core, gy, turn(yl, k, yls) * xs + xx)
        for h in range(yhs)
        for k in range(yls)
        if h or k
    ]
    group_c = [(gx, turn(gy, k, ny), gz) for k in range(1, ny)]
    reach = 4
    if ny > 2 * reach + 1:
        near = [(gx, turn(gy, s * k, ny), gz) for k in range(1, reach + 1) for s in (1, -1)]
    else:
        near = group_c
    greet = beside + group_a + group_b + near

    barrier = pltpu.get_barrier_semaphore()
    for device in greet:
        pl.semaphore_signal(barrier, inc=1, device_id=device, device_id_type=MESH)

    loads = [
        pltpu.make_async_copy(zones, own_zone, load_sem.at[0]),
        pltpu.make_async_copy(drained, own_drain, load_sem.at[1]),
        pltpu.make_async_copy(press_old, xu.at[0, 4:12, 8:24, :], load_sem.at[2]),
        pltpu.make_async_copy(motion_old, xu.at[1:4, 4:12, 8:24, :], load_sem.at[3]),
        pltpu.make_async_copy(source, own_src, load_sem.at[4]),
        pltpu.make_async_copy(strain_prev, own_strain, load_sem.at[5]),
        pltpu.make_async_copy(body_force, own_bf, load_sem.at[6]),
    ]
    for copy in loads:
        copy.start()

    def clear(ref):
        count = ref.shape[0]

        @pl.loop(0, 18)
        def _(i):
            for f in range(count):
                ref[f, i, 0:8, :] = jnp.zeros((8, 128), F32)
                ref[f, i, 24:32, :] = jnp.zeros((8, 128), F32)

    for ref in (zd, xu, z0, ze, mat, tf, mf, sp, gv, se, mo):
        clear(ref)
    wide = (zd, xu, z0, ze)

    @pl.when(jnp.logical_not(x_lo))
    def _():
        for ref in wide:
            ref[:, 0:4, 8:24, :] = jnp.zeros((ref.shape[0], 4, 16, 128), F32)

    @pl.when(jnp.logical_not(x_hi))
    def _():
        for ref in wide:
            ref[:, 12:16, 8:24, :] = jnp.zeros((ref.shape[0], 4, 16, 128), F32)

    @pl.when(jnp.logical_not(z_lo))
    def _():
        for ref in (pl_zd, pl_xu, pl_z0, pl_ze):
            ref[...] = jnp.zeros(ref.shape, F32)

    @pl.when(jnp.logical_not(z_hi))
    def _():
        for ref in (pr_zd, pr_xu, pr_z0, pr_ze):
            ref[...] = jnp.zeros(ref.shape, F32)

    rows[...] = jnp.zeros((32, 128), F32)
    loads[0].wait()
    loads[1].wait()
    zd[0, 4:12, 8:24, :] = own_zone[...].astype(F32) + 1.0
    zd[1, 4:12, 8:24, :] = own_drain[...].astype(F32)
    loads[2].wait()
    loads[3].wait()

    pl.semaphore_wait(barrier, len(greet))
    if ny > 2 * reach + 1:
        for by in (reach, -reach):
            pl.semaphore_signal(
                known, inc=1, device_id=(gx, turn(gy, by, ny), gz), device_id_type=MESH
            )

    def both(has_lo, has_hi, down, up):
        @pl.when(has_lo)
        def _():
            for copy in down:
                copy.start()

        @pl.when(has_hi)
        def _():
            for copy in up:
                copy.start()

        @pl.when(has_lo)
        def _():
            for copy_up, copy_down in zip(up, down):
                copy_down.wait_send()
                copy_up.wait_recv()

        @pl.when(has_hi)
        def _():
            for copy_up, copy_down in zip(up, down):
                copy_up.wait_send()
                copy_down.wait_recv()

    def send(src, dst, sems, slot, device):
        return pltpu.make_async_remote_copy(
            src_ref=src,
            dst_ref=dst,
            send_sem=sems[0].at[slot],
            recv_sem=sems[1].at[slot],
            device_id=device,
            device_id_type=MESH,
        )

    def exchange(fields, slot):
        down, up = ([], [])
        s = slot
        for ref, n, d, *_ in fields:
            some = pl.ds(0, n)
            down.append(
                send(
                    ref.at[some, pl.ds(4, d), pl.ds(8, 16), :],
                    ref.at[some, pl.ds(12, d), pl.ds(8, 16), :],
                    (xs_sem, xr_sem),
                    s,
                    (gx - 1, gy, gz),
                )
            )
            up.append(
                send(
                    ref.at[some, pl.ds(12 - d, d), pl.ds(8, 16), :],
                    ref.at[some, pl.ds(4 - d, d), pl.ds(8, 16), :],
                    (xs_sem, xr_sem),
                    s + 1,
                    (gx + 1, gy, gz),
                )
            )
            s += 2
        both(x_lo, x_hi, down, up)

        block = lax.broadcasted_iota(jnp.int32, (16, 128), 1) // 8
        down, up = ([], [])
        s = slot
        for ref, n, d, pack, left, right, *_ in fields:
            for f in range(n):
                packed = jnp.zeros((16, 128), F32)
                for i in range(4 - d, 12 + d):
                    turned = pltpu.roll(ref[f, i, 8:24, :], (8 * i + 4) % 128, 1)
                    packed = jnp.where(block == i, turned, packed)
                pack[f] = packed
            down.append(send(pack, right, (zs_sem, zr_sem), s, (gx, gy, gz - 1)))
            up.append(send(pack, left, (zs_sem, zr_sem), s + 1, (gx, gy, gz + 1)))
            s += 2
        both(z_lo, z_hi, down, up)
        low_half = lax.rem(lax.broadcasted_iota(jnp.int32, (16, 128), 1), 8) < 4
        for ref, n, d, pack, left, right, *_ in fields:
            for f in range(n):
                ref[f, L, 8:24, :] = jnp.where(low_half, left[f], pack[f])
                ref[f, R, 8:24, :] = jnp.where(low_half, pack[f], right[f])

        down, up = ([], [])
        s = slot
        for ref, n, d, pack, left, right, ys, yr in fields:
            span = 8 + 2 * d
            ys[0, :, 0:span] = ref[0:n, 4 - d : 12 + d, 8 : 8 + d, :]
            ys[0, :, span : span + 2] = ref[0:n, 16:18, 8 : 8 + d, :]
            ys[1, :, 0:span] = ref[0:n, 4 - d : 12 + d, 24 - d : 24, :]
            ys[1, :, span : span + 2] = ref[0:n, 16:18, 24 - d : 24, :]
            down.append(send(ys.at[0], yr.at[1], (yss_sem, yrs_sem), s, (gx, gy - 1, gz)))
            up.append(send(ys.at[1], yr.at[0], (yss_sem, yrs_sem), s + 1, (gx, gy + 1, gz)))
            s += 2
        both(y_lo, y_hi, down, up)

        @pl.when(y_lo)
        def _():
            for ref, n, d, pack, left, right, ys, yr in fields:
                span = 8 + 2 * d
                ref[0:n, 4 - d : 12 + d, 8 - d : 8, :] = yr[0, :, 0:span]
                ref[0:n, 16:18, 8 - d : 8, :] = yr[0, :, span : span + 2]

        @pl.when(y_hi)
        def _():
            for ref, n, d, pack, left, right, ys, yr in fields:
                span = 8 + 2 * d
                ref[0:n, 4 - d : 12 + d, 24 : 24 + d, :] = yr[1, :, 0:span]
                ref[0:n, 16:18, 24 : 24 + d, :] = yr[1, :, span : span + 2]

    exchange(
        [
            (xu, 4, 1, pk_xu, pl_xu, pr_xu, ys_xu, yr_xu),
            (zd, 2, 4, pk_zd, pl_zd, pr_zd, ys_zd, yr_zd),
        ],
        0,
    )

    def materials(row):
        zone = row.at(zd, 0)
        inside = zone > 0.5
        perm = jnp.zeros(zone.shape, F32)
        lame, shear = (perm, perm)
        for k in range(ZONES):
            hit = zone == k + 1.0
            perm = jnp.where(hit, perm_t[k], perm)
            lame = jnp.where(hit, lame_t[k], lame)
            shear = jnp.where(hit, shear_t[k], shear)
        bulk = jnp.where(inside, lame + 2.0 * shear / 3.0, 1.0)
        row.put(mat, 0, perm)
        row.put(mat, 1, lame + shear)
        row.put(mat, 2, shear)
        row.put(mat, 3, 0.2 + 0.64 / bulk + 2.0 * row.at(zd, 1))

    over_rows(0, 16, materials)

    def faces(row):
        for ref, f in ((tf, 0), (mf, 2)):
            own = row.at(mat, f)
            row.put(ref, 0, harmonic(own, row.xp(mat, f)))
            row.put(ref, 1, harmonic(own, row.yp(mat, f)))
            row.put(ref, 2, harmonic(own, row.zp(mat, f)))
            row.put(ref, 3, harmonic(own, row.zm(mat, f)))

    over_rows(0, 15, faces)

    def six(row, ref):
        return (
            row.at(ref, 0),
            row.xm(ref, 0),
            row.at(ref, 1),
            row.ym(ref, 1),
            row.at(ref, 2),
            row.at(ref, 3),
        )

    def around(row, ref, f):
        return (
            row.xp(ref, f),
            row.xm(ref, f),
            row.yp(ref, f),
            row.ym(ref, f),
            row.zp(ref, f),
            row.zm(ref, f),
        )

    def spread(factors, center, nearby):
        return sum(t * (center - v) for t, v in zip(factors, nearby))

    def diagonals(row):
        total = row.at(mat, 3) + sum(six(row, tf))
        row.put(diag, 0, total)
        row.put(diag, 1, 1.0 / total)
        heft = row.at(mat, 1)
        base = 1.0 + sum(six(row, mf)) + heft
        inside = row.at(mat, 2) > 0.0
        for c, other in enumerate((row.xm(mat, 1), row.ym(mat, 1), row.zm(mat, 1))):
            value = base + other
            row.put(ediag, c, value)
            row.put(ediag, 3 + c, jnp.where(inside, 1.0 / value, 0.0))

    over_rows(1, 15, diagonals)

    def divergence(row, ref, f):
        return (
            row.xp(ref, f)
            - row.at(ref, f)
            + (row.yp(ref, f + 1) - row.at(ref, f + 1))
            + (row.zp(ref, f + 2) - row.at(ref, f + 2))
        )

    def elastic(row, ref, f, g):
        factors = six(row, mf)
        own = row.at(gv, g)
        before = (row.xm(gv, g), row.ym(gv, g), row.zm(gv, g))
        done = []
        for c in range(3):
            center = row.at(ref, f + c)
            done.append(
                center + spread(factors, center, around(row, ref, f + c)) + (before[c] - own)
            )
        return done

    def old_scaled(row):
        row.put(gv, 0, row.at(mat, 1) * divergence(row, xu, 1))

    over_rows(3, 12, old_scaled, strips=(L,))

    for copy in loads[4:]:
        copy.wait()

    def first(row):
        j = row.i - 4
        x0 = row.at(xu, 0)
        nearby = around(row, xu, 0)
        central = 0.5 * (
            row.xp(xu, 1)
            - row.xm(xu, 1)
            + (row.yp(xu, 2) - row.ym(xu, 2))
            + (row.zp(xu, 3) - row.zm(xu, 3))
        )
        residual = (
            own_src[j]
            - 2.0 * row.at(zd, 1) * x0
            - 0.8 * (central - own_strain[j])
            - spread(six(row, tf), x0, nearby)
        )
        row.put(z0, 0, residual * row.at(diag, 1))
        image = elastic(row, xu, 1, 0)
        for c in range(3):
            force = own_bf[c, j] - image[c] - 0.4 * (nearby[2 * c] - nearby[2 * c + 1])
            row.put(ze, c, force * row.at(ediag, 3 + c))

    over_rows(4, 12, first, OWN, ())

    exchange(
        [
            (z0, 1, 4, pk_z0, pl_z0, pr_z0, ys_z0, yr_z0),
            (ze, 3, 2, pk_ze, pl_ze, pr_ze, ys_ze, yr_ze),
        ],
        4,
    )

    def second(row):
        center = row.at(z0, 0)
        image = row.at(mat, 3) * center + spread(six(row, tf), center, around(row, z0, 0))
        row.put(sp, 0, image * row.at(diag, 1))

    over_rows(1, 15, second)

    def basis(row):
        for p, ref in ((1, z0), (2, sp)):
            nearby = around(row, ref, 0)
            for c in range(3):
                force = -0.4 * (nearby[2 * c] - nearby[2 * c + 1])
                row.put(ze, 3 * p + c, force * row.at(ediag, 3 + c))

    over_rows(2, 14, basis)

    def scaled(row):
        heft = row.at(mat, 1)
        for p in range(3):
            row.put(gv, p, heft * divergence(row, ze, 3 * p))

    over_rows(2, 13, scaled)

    def images(row):
        for p in range(3):
            done = elastic(row, ze, 3 * p, p)
            for c in range(3):
                row.put(se, 3 * p + c, done[c] * row.at(ediag, 3 + c))

    over_rows(3, 13, images)

    zero = jnp.zeros((8, 128), F32)
    pairs = [(p, q) for p in range(3) for q in range(p, 3)]

    def pressure_moments(i, sums):
        row = Row(i, OWN, False)
        z, s, d = (row.at(z0, 0), row.at(sp, 0), row.at(diag, 0))
        dz, ds = (d * z, d * s)
        energy = row.at(mat, 3) * s * s
        for f, other in enumerate((row.xp(sp, 0), row.yp(sp, 0), row.zp(sp, 0))):
            gap = s - other
            energy = energy + row.at(tf, f) * gap * gap
        new = (dz * z, dz * s, ds * s, energy)
        return tuple(a + fold(b) for a, b in zip(sums, new))

    def plain_moments(i, sums):
        row = Row(i, OWN, False)
        new = [None] * 18

        def add(k, value):
            new[k] = value if new[k] is None else new[k] + value

        for c in range(3):
            d = row.at(ediag, c)
            g = [row.at(ze, 3 * p + c) for p in range(3)]
            s = [row.at(se, 3 * p + c) for p in range(3)]
            dg = [d * v for v in g]
            ds = [d * v for v in s]
            for k, (p, q) in enumerate(pairs):
                add(k, dg[p] * g[q])
                add(6 + k, dg[p] * s[q])
                add(12 + k, ds[p] * s[q])
        return tuple(a + fold(b) for a, b in zip(sums, new))

    def energy_moments(i, sums):
        row = Row(i, OWN, False)
        new = [jnp.zeros((16, 128), F32)] * 6
        heft = row.at(mat, 1)
        factors = [row.at(mf, f) for f in range(3)]
        div = [None] * 3
        for c in range(3):
            s = [row.at(se, 3 * p + c) for p in range(3)]
            for k, (p, q) in enumerate(pairs):
                new[k] = new[k] + s[p] * s[q]
            for f, pick in enumerate((row.xp, row.yp, row.zp)):
                gap = [pick(se, 3 * p + c) - s[p] for p in range(3)]
                if f == c:
                    div = [g if d is None else d + g for d, g in zip(div, gap)]
                scaled_gap = [factors[f] * g for g in gap]
                for k, (p, q) in enumerate(pairs):
                    new[k] = new[k] + scaled_gap[p] * gap[q]
        for k, (p, q) in enumerate(pairs):
            new[k] = new[k] + heft * div[p] * div[q]
        return tuple(a + fold(b) for a, b in zip(sums, new))

    sums = lax.fori_loop(4, 12, pressure_moments, (zero,) * 4)
    sums += lax.fori_loop(4, 12, plain_moments, (zero,) * 18)
    sums += lax.fori_loop(4, 12, energy_moments, (zero,) * 6)
    for k, value in enumerate(sums):
        rows[k : k + 1, :] = jnp.sum(value, axis=0, keepdims=True)
    eye = lax.broadcasted_iota(jnp.int32, (32, 128), 0) == lax.broadcasted_iota(
        jnp.int32, (32, 128), 1
    )
    column = jnp.sum(rows[...], axis=1, keepdims=True)
    part[0] = jnp.sum(jnp.where(eye, column, 0.0), axis=0, keepdims=True)

    slot = 0
    for stage, (group, got) in enumerate(((group_a, got_a), (group_b, got_b), (group_c, got_c))):
        if stage == 2 and ny > 2 * reach + 1:
            pl.semaphore_wait(known, 2)
        copies = []
        for k, device in enumerate(group):
            copies.append(send(part.at[stage], got.at[k], (rs_sem, rr_sem), slot + k, device))
        slot += len(group)
        for copy in copies:
            copy.start()
        for copy in copies:
            copy.wait()
        total = part[stage]
        for k in range(len(group)):
            total = total + got[k]
        part[stage + 1] = total

    column = jnp.sum(jnp.where(eye, part[3], 0.0), axis=1, keepdims=True)
    m = [column[k : k + 1, :] for k in range(28)]

    def steps(m0, m1, m2, m3):
        alpha = m0 / m1
        gamma = m0 - 2.0 * alpha * m1 + alpha * alpha * m2
        delta = m1 - 2.0 * alpha * m2 + alpha * alpha * m3
        beta = gamma / m0
        step = gamma / (delta - beta * gamma / alpha)
        return (alpha + step * (1.0 + beta), -alpha * step)

    a, b = steps(*m[0:4])

    def quadratic(v):
        return v[0] + 2.0 * (a * v[1] + b * v[2]) + a * a * v[3] + 2.0 * a * b * v[4] + b * b * v[5]

    ea, eb = steps(*[quadratic(m[4 + 6 * k : 10 + 6 * k]) for k in range(4)])

    def moved(row):
        for c in range(3):
            z = row.at(ze, c) + a * row.at(ze, 3 + c) + b * row.at(ze, 6 + c)
            s = row.at(se, c) + a * row.at(se, 3 + c) + b * row.at(se, 6 + c)
            row.put(mo, c, row.at(xu, 1 + c) + ea * z + eb * s)

    over_rows(3, 13, moved)

    def finish(row):
        j = row.i - 4
        press_out[j] = row.at(xu, 0) + a * row.at(z0, 0) + b * row.at(sp, 0)
        for c in range(3):
            motion_out[c, j] = row.at(mo, c)
        strain_out[j] = 0.5 * (
            row.xp(mo, 0)
            - row.xm(mo, 0)
            + (row.yp(mo, 1) - row.ym(mo, 1))
            + (row.zp(mo, 2) - row.zm(mo, 2))
        )

    over_rows(4, 12, finish, OWN, ())


def local_step(sizes, *args):
    nx, ny, nz, cores, xs = sizes

    def field(n):
        return pltpu.VMEM((n, 18, 32, 128), F32)

    def vmem(*shape):
        return pltpu.VMEM(shape, F32)

    moving = ((2, 4), (4, 1), (1, 4), (3, 2))
    packs = [vmem(n, 16, 128) for n, _ in moving]
    y_parts = [vmem(2, n, 10 + 2 * d, d, 128) for n, d in moving]
    group_a, group_b, group_c = (cores * xs, (nx // cores) * (nz // xs), ny)
    sent = group_a + group_b + group_c - 3
    dma = pltpu.SemaphoreType.DMA
    scratch = [
        vmem(8, 16, 128),
        vmem(8, 16, 128),
        vmem(3, 8, 16, 128),
        pltpu.VMEM((8, 16, 128), jnp.int32),
        pltpu.VMEM((8, 16, 128), jnp.int32),
        field(2),
        field(4),
        field(1),
        field(9),
        field(4),
        field(4),
        field(4),
        field(2),
        field(6),
        field(1),
        field(3),
        field(9),
        field(3),
        *packs,
        *packs,
        *packs,
        *y_parts,
        *y_parts,
        vmem(32, 128),
        vmem(4, 1, 128),
        vmem(max(group_a - 1, 1), 1, 128),
        vmem(max(group_b - 1, 1), 1, 128),
        vmem(max(group_c - 1, 1), 1, 128),
        dma((7,)),
        *[dma((8,)) for _ in range(6)],
        dma((max(sent, 1),)),
        dma((max(sent, 1),)),
        pltpu.SemaphoreType.REGULAR,
    ]
    anywhere = pl.BlockSpec(memory_space=pl.ANY)
    scalars = pl.BlockSpec(memory_space=pltpu.SMEM)
    near = pl.BlockSpec(memory_space=pltpu.VMEM)
    return pl.pallas_call(
        functools.partial(kernel, sizes),
        name="biot_step",
        out_shape=(
            jax.ShapeDtypeStruct((8, 16, 128), F32),
            jax.ShapeDtypeStruct((3, 8, 16, 128), F32),
            jax.ShapeDtypeStruct((8, 16, 128), F32),
        ),
        in_specs=[anywhere] * 7 + [scalars] * 3,
        out_specs=(near, near, near),
        scratch_shapes=scratch,
        compiler_params=pltpu.CompilerParams(
            collective_id=0, has_side_effects=True, vmem_limit_bytes=48 * 1024 * 1024
        ),
    )(*args)


def solution(mesh, cores=2, xs=4):
    sizes = (mesh.shape["gx"], mesh.shape["gy"], mesh.shape["gz"], cores, xs)
    scalar = P("gx", "gy", "gz")
    vector = P(None, "gx", "gy", "gz")
    return jax.shard_map(
        functools.partial(local_step, sizes),
        mesh=mesh,
        in_specs=(scalar, scalar, scalar, vector, vector, scalar, scalar, P(), P(), P()),
        out_specs=(scalar, vector, scalar),
        check_vma=False,
    )
```

time: 481 us -> 89.8 us (0.19)
  the two profiles are of different devices: /device:TPU:8 before, /device:TPU:1 now
where the time goes in v1:
time: 89.8 us; the launch traced here: 89.1 us
  Pallas kernels  78.5 us (87%)
  local copies, waits for them, and re-layouts  9.94 us (11%)
    pallas_call x1, Pallas kernels, local_step(): pl.pallas_call(functools.partial(kernel, sizes), name='biot_step', out_sh...  78.5 us
    unnamed x23, local copies, waits for them, and re-layouts  9.94 us

profile of v1, /device:TPU:1, one launch (start us, length us, event | category | flops | bytes accessed | tf_op | source)
XLA Modules:
  0.0 89.1 jit_solution(17087160095364785024)
XLA Ops:
  0.6 0.0 copy-start
  0.6 0.9 %copy-done = f32[3,8,16,128]{3,2,1,0:T(8,128)S(1)} copy-done((f32[3,8,16,128]{3,2,1,0:T(8,128)S(1)}, f32[3,8,16,128]{3,2,1,0:T(8,128)}, u32[]{:S(2)}) %copy-start) | copy-done | bytes 196632
  1.6 0.0 copy-start.1
  1.6 0.9 %copy-done.1 = f32[3,8,16,128]{3,2,1,0:T(8,128)S(1)} copy-done((f32[3,8,16,128]{3,2,1,0:T(8,128)S(1)}, f32[3,8,16,128]{3,2,1,0:T(8,128)}, u32[]{:S(2)}) %copy-start.1) | copy-done | bytes 196632
  2.5 0.0 copy-start.2
  2.5 0.8 copy-done.2
  3.3 0.0 copy-start.3
  3.3 0.8 copy-done.3
  4.2 0.0 copy-start.4
  4.2 0.8 copy-done.4
  5.0 0.0 copy-start.5
  5.0 0.8 copy-done.5
  5.8 0.0 copy-start.6
  5.9 0.8 copy-done.6
  6.7 0.0 copy-start.7
  6.7 0.7 copy-done.7
  7.3 0.0 copy-start.8
  7.3 0.7 copy-done.8
  8.0 0.0 copy-start.9
  8.0 0.7 copy-done.9
  8.7 78.5 %biot_step.1 = (f32[8,16,128]{2,1,0:T(8,128)S(1)}, f32[3,8,16,128]{3,2,1,0:T(8,128)S(1)}, f32[8,16,128]{2,1,0:T(8,128)S(1)}) custom-call(f32[8,16,128]{2,1,0:T(8,128)S(1)} %copy-done.2, f32[8,16,128]{2,1,0:T(8,128)S(1)} %copy-done.3, f32[8,16,128]{2,1,0:T(8,128)S(1)} %copy-done.4, f32[3,8,16,128]{3,2,1,0:T(8,128)S(1)} %copy-done, ...), custom_call_target="tpu_custom_call" | custom-call | tf_op jit(solution)/shard_map/biot_step/pallas_call | solution.py:705
  87.1 0.6 copy.16
  87.8 0.7 copy.17
  88.4 0.6 copy.18
Async XLA Ops:
  0.6 0.9 %copy-start = (f32[3,8,16,128]{3,2,1,0:T(8,128)S(1)}, f32[3,8,16,128]{3,2,1,0:T(8,128)}, u32[]{:S(2)}) copy-start(f32[3,8,16,128]{3,2,1,0:T(8,128)} %motion_old.1) | copy-start | bytes 589828
  1.6 0.9 %copy-start.1 = (f32[3,8,16,128]{3,2,1,0:T(8,128)S(1)}, f32[3,8,16,128]{3,2,1,0:T(8,128)}, u32[]{:S(2)}) copy-start(f32[3,8,16,128]{3,2,1,0:T(8,128)} %body_force.1) | copy-start | bytes 589828
  2.5 0.8 copy-start.2
  3.3 0.8 copy-start.3
  4.2 0.8 copy-start.4
  5.0 0.8 copy-start.5
  5.8 0.8 copy-start.6
  6.7 0.7 copy-start.7
  7.3 0.7 copy-start.8
  8.0 0.7 copy-start.9

commit v2 on v1

--- a/solution.py
+++ b/solution.py
@@ -63,13 +63,13 @@
 
 
 def over_rows(low, high, body, window=WIN, strips=(L, R)):
-    @pl.loop(low, high)
+    @pl.loop(low, high, unroll=min(4, high - low))
     def _(i):
         body(Row(i, window, False))
 
     if strips:
 
-        @pl.loop(strips[0], strips[-1] + 1)
+        @pl.loop(strips[0], strips[-1] + 1, unroll=True)
         def _(i):
             body(Row(i, window, True))
 
@@ -92,12 +92,15 @@
     body_force,
     zones,
     drained,
+    perm_h,
+    lame_h,
+    shear_h,
+    press_out,
+    motion_out,
+    strain_out,
     perm_t,
     lame_t,
     shear_t,
-    press_out,
-    motion_out,
-    strain_out,
     own_src,
     own_strain,
     own_bf,
@@ -116,38 +119,23 @@
     gv,
     se,
     mo,
-    pk_zd,
-    pk_xu,
-    pk_z0,
-    pk_ze,
-    pl_zd,
-    pl_xu,
-    pl_z0,
-    pl_ze,
-    pr_zd,
-    pr_xu,
-    pr_z0,
-    pr_ze,
+    ys_xu,
     ys_zd,
-    ys_xu,
     ys_z0,
     ys_ze,
+    yr_xu,
     yr_zd,
-    yr_xu,
     yr_z0,
     yr_ze,
+    strips_1,
+    strips_2,
     rows,
     part,
     got_a,
     got_b,
-    got_c,
     load_sem,
-    xs_sem,
-    xr_sem,
-    zs_sem,
-    zr_sem,
-    yss_sem,
-    yrs_sem,
+    hs_sem,
+    hr_sem,
     rs_sem,
     rr_sem,
     known,
@@ -158,60 +146,304 @@
     x_lo, x_hi = (gx > 0, gx < nx - 1)
     y_lo, y_hi = (gy > 0, gy < ny - 1)
     z_lo, z_hi = (gz > 0, gz < nz - 1)
+    axes = ((x_lo, x_hi, nx), (y_lo, y_hi, ny), (z_lo, z_hi, nz))
 
     def turn(value, by, count):
         return lax.rem(value + (by % count), count)
 
-    beside = []
-    for by in (1, -1):
-        if nx > 1:
-            beside.append((turn(gx, by, nx), gy, gz))
-        if ny > 1:
-            beside.append((gx, turn(gy, by, ny), gz))
-        if nz > 1:
-            beside.append((gx, gy, turn(gz, by, nz)))
+    ways = [
+        (dx, dy, dz)
+        for dx in (1, -1, 0)
+        for dy in (1, -1, 0)
+        for dz in (1, -1, 0)
+        if dx or dy or dz
+    ]
+    ways = [w for w in ways if all(count > 1 or not step for step, (_, _, count) in zip(w, axes))]
+
+    def there(way):
+        ok = None
+        for step, (low, high, _) in zip(way, axes):
+            if step:
+                side = high if step > 0 else low
+                ok = side if ok is None else jnp.logical_and(ok, side)
+        return ok
+
+    def device(way):
+        return (gx + way[0], gy + way[1], gz + way[2])
+
     yh, core = (gx // cores, lax.rem(gx, cores))
     yl, xx = (gz // xs, lax.rem(gz, xs))
     group_a = [
-        (yh * cores + turn(core, c, cores), gy, yl * xs + turn(xx, x, xs))
-        for c in range(cores)
-        for x in range(xs)
-        if c or x
-    ]
-    group_b = [
-        (turn(yh, h, yhs) * cores + core, gy, turn(yl, k, yls) * xs + xx)
+        (turn(yh, h, yhs) * cores + core, gy, turn(yl, k, yls) * xs + turn(xx, x, xs))
         for h in range(yhs)
         for k in range(yls)
-        if h or k
+        for x in range(xs)
+        if h or k or x
     ]
-    group_c = [(gx, turn(gy, k, ny), gz) for k in range(1, ny)]
     reach = 4
-    if ny > 2 * reach + 1:
-        near = [(gx, turn(gy, s * k, ny), gz) for k in range(1, reach + 1) for s in (1, -1)]
+    chained = ny > 2 * reach + 1
+
+    def over_z(k, c):
+        return (yh * cores + turn(core, c, cores), turn(gy, k, ny), gz)
+
+    group_b = [over_z(k, c) for k in range(ny) for c in range(cores) if k or c]
+    if chained:
+        near = [
+            over_z(k, c)
+            for k in range(-reach, reach + 1)
+            for c in range(cores)
+            if k or c
+        ]
     else:
-        near = group_c
-    greet = beside + group_a + group_b + near
+        near = group_b
 
     barrier = pltpu.get_barrier_semaphore()
-    for device in greet:
-        pl.semaphore_signal(barrier, inc=1, device_id=device, device_id_type=MESH)
+    for way in ways:
+
+        @pl.when(there(way))
+        def _(way=way):
+            pl.semaphore_signal(barrier, inc=1, device_id=device(way), device_id_type=MESH)
+
+    for other in group_a + near:
+        pl.semaphore_signal(barrier, inc=1, device_id=other, device_id_type=MESH)
 
     loads = [
-        pltpu.make_async_copy(zones, own_zone, load_sem.at[0]),
-        pltpu.make_async_copy(drained, own_drain, load_sem.at[1]),
-        pltpu.make_async_copy(press_old, xu.at[0, 4:12, 8:24, :], load_sem.at[2]),
-        pltpu.make_async_copy(motion_old, xu.at[1:4, 4:12, 8:24, :], load_sem.at[3]),
-        pltpu.make_async_copy(source, own_src, load_sem.at[4]),
-        pltpu.make_async_copy(strain_prev, own_strain, load_sem.at[5]),
-        pltpu.make_async_copy(body_force, own_bf, load_sem.at[6]),
+        pltpu.make_async_copy(src, dst, load_sem.at[k])
+        for k, (src, dst) in enumerate(
+            (
+                (zones, own_zone),
+                (drained, own_drain),
+                (press_old, xu.at[0, 4:12, 8:24, :]),
+                (motion_old, xu.at[1:4, 4:12, 8:24, :]),
+                (source, own_src),
+                (strain_prev, own_strain),
+                (body_force, own_bf),
+                (perm_h, perm_t),
+                (lame_h, lame_t),
+                (shear_h, shear_t),
+            )
+        )
     ]
     for copy in loads:
         copy.start()
 
+    def send(src, dst, slot, to):
+        return pltpu.make_async_remote_copy(
+            src_ref=src,
+            dst_ref=dst,
+            send_sem=hs_sem.at[slot],
+            recv_sem=hr_sem.at[slot],
+            device_id=to,
+            device_id_type=MESH,
+        )
+
+    lane = lanes(16)
+    block = lane // 8
+    quarter = lane // 32
+    low_half = lax.rem(lane, 8) < 4
+
+    def side(step):
+        return (1, 0) if step > 0 else (0, 1)
+
+    class Exchange:
+        def __init__(self, groups, strips, slot):
+            self.groups = groups
+            self.pk, self.px, self.py, self.pxy, self.rz, self.rxz, self.ryz, self.rxyz = strips
+            self.fields = [(ref, f) for ref, n, *_ in groups for f in range(n)]
+            self.copies = {}
+            for way in ways:
+                dx, dy, dz = way
+                pairs = []
+                if dz:
+                    out, come = side(dz)
+                    a, b = (side(dx) if dx else (0, 0), side(dy) if dy else (0, 0))
+                    if dx and dy:
+                        pairs.append((self.pxy.at[a[0], b[0]], self.rxyz.at[come, a[1], b[1]]))
+                    elif dx:
+                        pairs.append((self.px.at[a[0]], self.rxz.at[come, a[1]]))
+                    elif dy:
+                        pairs.append((self.py.at[b[0]], self.ryz.at[come, b[1]]))
+                    else:
+                        pairs.append((self.pk, self.rz.at[come]))
+                else:
+                    for ref, n, d, ys, yr in groups:
+                        if dx:
+                            first = 8 - d if dx > 0 else 0
+                            put = 0 if dx > 0 else 8 + d
+                        if dx and not dy:
+                            x_from, x_to = (4 + first, 4 - d + put)
+                            some = pl.ds(0, n)
+                            pairs.append(
+                                (
+                                    ref.at[some, pl.ds(x_from, d), pl.ds(8, 16), :],
+                                    ref.at[some, pl.ds(x_to, d), pl.ds(8, 16), :],
+                                )
+                            )
+                        elif dx:
+                            b = side(dy)
+                            pairs.append(
+                                (
+                                    ys.at[b[0], :, pl.ds(first, d)],
+                                    yr.at[b[1], :, pl.ds(put, d)],
+                                )
+                            )
+                        else:
+                            b = side(dy)
+                            pairs.append((ys.at[b[0]], yr.at[b[1], :, pl.ds(d, 8)]))
+                self.copies[way] = [
+                    send(src, dst, slot + k, device(way)) for k, (src, dst) in enumerate(pairs)
+                ]
+                slot += len(pairs)
+
+        def pack(self):
+            for ref, n, d, ys, yr in self.groups:
+                ys[0] = ref[0:n, 4:12, 8 : 8 + d, :]
+                ys[1] = ref[0:n, 4:12, 24 - d : 24, :]
+            count = self.px.shape[1]
+            across = [[jnp.zeros((16, 128), F32) for _ in range(count)] for _ in range(2)]
+            for k, (ref, f) in enumerate(self.fields):
+                packed = jnp.zeros((16, 128), F32)
+                for i in range(4, 12):
+                    turned = pltpu.roll(ref[f, i, 8:24, :], (8 * i + 4) % 128, 1)
+                    packed = jnp.where(block == i, turned, packed)
+                self.pk[k] = packed
+                self.py[0, k] = packed[0:4]
+                self.py[1, k] = packed[12:16]
+                q, g = (k % 4, k // 4)
+                for s, base in ((0, 32), (1, 64)):
+                    turned = pltpu.roll(packed, (32 * q - base) % 128, 1)
+                    across[s][g] = jnp.where(quarter == q, turned, across[s][g])
+            for s in range(2):
+                for g in range(count):
+                    self.px[s, g] = across[s][g]
+                    self.pxy[s, 0, g] = across[s][g][0:4]
+                    self.pxy[s, 1, g] = across[s][g][12:16]
+
+        def start(self):
+            for way in ways:
+
+                @pl.when(there(way))
+                def _(way=way):
+                    for copy in self.copies[way]:
+                        copy.start()
+
+        def blank(self):
+            for s, have in ((0, x_lo), (1, x_hi)):
+
+                @pl.when(jnp.logical_not(have))
+                def _(s=s):
+                    for ref, n, d, ys, yr in self.groups:
+                        ref[0:n, 12 * s : 12 * s + 4, 8:24, :] = jnp.zeros((n, 4, 16, 128), F32)
+                        for y in range(2):
+                            at = (8 + d) * s
+                            yr[y, :, at : at + d] = jnp.zeros((n, d, d, 128), F32)
+                    for z in range(2):
+                        self.rxz[z, s] = jnp.zeros(self.rxz.shape[2:], F32)
+                        self.rxyz[z, s] = jnp.zeros(self.rxyz.shape[2:], F32)
+
+            for s, have in ((0, y_lo), (1, y_hi)):
+
+                @pl.when(jnp.logical_not(have))
+                def _(s=s):
+                    for z in range(2):
+                        self.ryz[z, s] = jnp.zeros(self.ryz.shape[2:], F32)
+                        for x in range(2):
+                            self.rxyz[z, x, s] = jnp.zeros(self.rxyz.shape[3:], F32)
+
+            for s, have in ((0, z_lo), (1, z_hi)):
+
+                @pl.when(jnp.logical_not(have))
+                def _(s=s):
+                    for ref in (self.rz, self.rxz, self.ryz, self.rxyz):
+                        ref[s] = jnp.zeros(ref.shape[1:], F32)
+
+        def arrived(self, some):
+            for way in some:
+
+                @pl.when(there(tuple(-step for step in way)))
+                def _(way=way):
+                    for copy in self.copies[way]:
+                        copy.wait_recv()
+
+        def finish(self):
+            self.arrived([way for way in ways if not way[2]])
+            for s, have in ((0, y_lo), (1, y_hi)):
+
+                @pl.when(have)
+                def _(s=s):
+                    for ref, n, d, ys, yr in self.groups:
+                        at = 24 if s else 8 - d
+                        ref[0:n, 4 - d : 12 + d, at : at + d, :] = yr[s]
+
+            wide = lanes(24) // 8
+            for ref, n, d, *_ in self.groups:
+                for f in range(n):
+                    packed = jnp.zeros((24, 128), F32)
+                    for i in range(4 - d, 12 + d):
+                        turned = pltpu.roll(ref[f, i, 4:28, :], (8 * i + 4) % 128, 1)
+                        packed = jnp.where(wide == i, turned, packed)
+                    ref[f, L, 4:28, :] = packed
+                    ref[f, R, 4:28, :] = packed
+            self.arrived([way for way in ways if way[2]])
+            for k, (ref, f) in enumerate(self.fields):
+                q, g = (k % 4, k // 4)
+                for z, strip in ((0, L), (1, R)):
+                    mine = low_half if z == 0 else jnp.logical_not(low_half)
+
+                    def joined(low, middle, high, count):
+                        here = lane[0:count]
+                        low = pltpu.roll(low, (-32 * q) % 128, 1)
+                        high = pltpu.roll(high, (96 - 32 * q) % 128, 1)
+                        return jnp.where(here < 32, low, jnp.where(here >= 96, high, middle))
+
+                    for start, count, got in (
+                        (8, 16, (self.rxz[z, 0, g], self.rz[z, k], self.rxz[z, 1, g])),
+                        (4, 4, (self.rxyz[z, 0, 0, g], self.ryz[z, 0, k], self.rxyz[z, 1, 0, g])),
+                        (24, 4, (self.rxyz[z, 0, 1, g], self.ryz[z, 1, k], self.rxyz[z, 1, 1, g])),
+                    ):
+                        own = ref[f, strip, start : start + count, :]
+                        ref[f, strip, start : start + count, :] = jnp.where(
+                            mine[0:count], joined(*got, count), own
+                        )
+            for way in ways:
+
+                @pl.when(there(way))
+                def _(way=way):
+                    for copy in self.copies[way]:
+                        copy.wait_send()
+
+    round_1 = Exchange(
+        [(xu, 4, 1, ys_xu, yr_xu), (zd, 2, 4, ys_zd, yr_zd)],
+        strips_1,
+        0,
+    )
+    slots_1 = sum(len(c) for c in round_1.copies.values())
+    round_2 = Exchange(
+        [(z0, 1, 4, ys_z0, yr_z0), (ze, 3, 2, ys_ze, yr_ze)],
+        strips_2,
+        slots_1,
+    )
+
+    for copy in loads[0:4]:
+        copy.wait()
+    zd[0, 4:12, 8:24, :] = own_zone[...].astype(F32) + 1.0
+    zd[1, 4:12, 8:24, :] = own_drain[...].astype(F32)
+    round_1.pack()
+    greeted = len(group_a) + len(near) - 1
+    around_here = None
+    for low, high, _ in axes:
+        count = 1 + low.astype(jnp.int32) + high.astype(jnp.int32)
+        around_here = count if around_here is None else around_here * count
+    pl.semaphore_wait(barrier, greeted + around_here)
+    round_1.start()
+    if chained:
+        for by in (reach, -reach):
+            pl.semaphore_signal(known, inc=1, device_id=over_z(by, 0), device_id_type=MESH)
+
     def clear(ref):
         count = ref.shape[0]
 
-        @pl.loop(0, 18)
+        @pl.loop(0, 18, unroll=3)
         def _(i):
             for f in range(count):
                 ref[f, i, 0:8, :] = jnp.zeros((8, 128), F32)
@@ -219,156 +451,12 @@
 
     for ref in (zd, xu, z0, ze, mat, tf, mf, sp, gv, se, mo):
         clear(ref)
-    wide = (zd, xu, z0, ze)
-
-    @pl.when(jnp.logical_not(x_lo))
-    def _():
-        for ref in wide:
-            ref[:, 0:4, 8:24, :] = jnp.zeros((ref.shape[0], 4, 16, 128), F32)
-
-    @pl.when(jnp.logical_not(x_hi))
-    def _():
-        for ref in wide:
-            ref[:, 12:16, 8:24, :] = jnp.zeros((ref.shape[0], 4, 16, 128), F32)
-
-    @pl.when(jnp.logical_not(z_lo))
-    def _():
-        for ref in (pl_zd, pl_xu, pl_z0, pl_ze):
-            ref[...] = jnp.zeros(ref.shape, F32)
-
-    @pl.when(jnp.logical_not(z_hi))
-    def _():
-        for ref in (pr_zd, pr_xu, pr_z0, pr_ze):
-            ref[...] = jnp.zeros(ref.shape, F32)
-
+    round_1.blank()
+    round_2.blank()
     rows[...] = jnp.zeros((32, 128), F32)
-    loads[0].wait()
-    loads[1].wait()
-    zd[0, 4:12, 8:24, :] = own_zone[...].astype(F32) + 1.0
-    zd[1, 4:12, 8:24, :] = own_drain[...].astype(F32)
-    loads[2].wait()
-    loads[3].wait()
-
-    pl.semaphore_wait(barrier, len(greet))
-    if ny > 2 * reach + 1:
-        for by in (reach, -reach):
-            pl.semaphore_signal(
-                known, inc=1, device_id=(gx, turn(gy, by, ny), gz), device_id_type=MESH
-            )
-
-    def both(has_lo, has_hi, down, up):
-        @pl.when(has_lo)
-        def _():
-            for copy in down:
-                copy.start()
-
-        @pl.when(has_hi)
-        def _():
-            for copy in up:
-                copy.start()
-
-        @pl.when(has_lo)
-        def _():
-            for copy_up, copy_down in zip(up, down):
-                copy_down.wait_send()
-                copy_up.wait_recv()
-
-        @pl.when(has_hi)
-        def _():
-            for copy_up, copy_down in zip(up, down):
-                copy_up.wait_send()
-                copy_down.wait_recv()
-
-    def send(src, dst, sems, slot, device):
-        return pltpu.make_async_remote_copy(
-            src_ref=src,
-            dst_ref=dst,
-            send_sem=sems[0].at[slot],
-            recv_sem=sems[1].at[slot],
-            device_id=device,
-            device_id_type=MESH,
-        )
-
-    def exchange(fields, slot):
-        down, up = ([], [])
-        s = slot
-        for ref, n, d, *_ in fields:
-            some = pl.ds(0, n)
-            down.append(
-                send(
-                    ref.at[some, pl.ds(4, d), pl.ds(8, 16), :],
-                    ref.at[some, pl.ds(12, d), pl.ds(8, 16), :],
-                    (xs_sem, xr_sem),
-                    s,
-                    (gx - 1, gy, gz),
-                )
-            )
-            up.append(
-                send(
-                    ref.at[some, pl.ds(12 - d, d), pl.ds(8, 16), :],
-                    ref.at[some, pl.ds(4 - d, d), pl.ds(8, 16), :],
-                    (xs_sem, xr_sem),
-                    s + 1,
-                    (gx + 1, gy, gz),
-                )
-            )
-            s += 2
-        both(x_lo, x_hi, down, up)
-
-        block = lax.broadcasted_iota(jnp.int32, (16, 128), 1) // 8
-        down, up = ([], [])
-        s = slot
-        for ref, n, d, pack, left, right, *_ in fields:
-            for f in range(n):
-                packed = jnp.zeros((16, 128), F32)
-                for i in range(4 - d, 12 + d):
-                    turned = pltpu.roll(ref[f, i, 8:24, :], (8 * i + 4) % 128, 1)
-                    packed = jnp.where(block == i, turned, packed)
-                pack[f] = packed
-            down.append(send(pack, right, (zs_sem, zr_sem), s, (gx, gy, gz - 1)))
-            up.append(send(pack, left, (zs_sem, zr_sem), s + 1, (gx, gy, gz + 1)))
-            s += 2
-        both(z_lo, z_hi, down, up)
-        low_half = lax.rem(lax.broadcasted_iota(jnp.int32, (16, 128), 1), 8) < 4
-        for ref, n, d, pack, left, right, *_ in fields:
-            for f in range(n):
-                ref[f, L, 8:24, :] = jnp.where(low_half, left[f], pack[f])
-                ref[f, R, 8:24, :] = jnp.where(low_half, pack[f], right[f])
-
-        down, up = ([], [])
-        s = slot
-        for ref, n, d, pack, left, right, ys, yr in fields:
-            span = 8 + 2 * d
-            ys[0, :, 0:span] = ref[0:n, 4 - d : 12 + d, 8 : 8 + d, :]
-            ys[0, :, span : span + 2] = ref[0:n, 16:18, 8 : 8 + d, :]
-            ys[1, :, 0:span] = ref[0:n, 4 - d : 12 + d, 24 - d : 24, :]
-            ys[1, :, span : span + 2] = ref[0:n, 16:18, 24 - d : 24, :]
-            down.append(send(ys.at[0], yr.at[1], (yss_sem, yrs_sem), s, (gx, gy - 1, gz)))
-            up.append(send(ys.at[1], yr.at[0], (yss_sem, yrs_sem), s + 1, (gx, gy + 1, gz)))
-            s += 2
-        both(y_lo, y_hi, down, up)
-
-        @pl.when(y_lo)
-        def _():
-            for ref, n, d, pack, left, right, ys, yr in fields:
-                span = 8 + 2 * d
-                ref[0:n, 4 - d : 12 + d, 8 - d : 8, :] = yr[0, :, 0:span]
-                ref[0:n, 16:18, 8 - d : 8, :] = yr[0, :, span : span + 2]
-
-        @pl.when(y_hi)
-        def _():
-            for ref, n, d, pack, left, right, ys, yr in fields:
-                span = 8 + 2 * d
-                ref[0:n, 4 - d : 12 + d, 24 : 24 + d, :] = yr[1, :, 0:span]
-                ref[0:n, 16:18, 24 : 24 + d, :] = yr[1, :, span : span + 2]
-
-    exchange(
-        [
-            (xu, 4, 1, pk_xu, pl_xu, pr_xu, ys_xu, yr_xu),
-            (zd, 2, 4, pk_zd, pl_zd, pr_zd, ys_zd, yr_zd),
-        ],
-        0,
-    )
+    for copy in loads[4:]:
+        copy.wait()
+    round_1.finish()
 
     def materials(row):
         zone = row.at(zd, 0)
@@ -386,7 +474,7 @@
         row.put(mat, 2, shear)
         row.put(mat, 3, 0.2 + 0.64 / bulk + 2.0 * row.at(zd, 1))
 
-    over_rows(0, 16, materials)
+    over_rows(3, 13, materials)
 
     def faces(row):
         for ref, f in ((tf, 0), (mf, 2)):
@@ -396,7 +484,7 @@
             row.put(ref, 2, harmonic(own, row.zp(mat, f)))
             row.put(ref, 3, harmonic(own, row.zm(mat, f)))
 
-    over_rows(0, 15, faces)
+    over_rows(3, 12, faces, strips=())
 
     def six(row, ref):
         return (
@@ -433,7 +521,7 @@
             row.put(ediag, c, value)
             row.put(ediag, 3 + c, jnp.where(inside, 1.0 / value, 0.0))
 
-    over_rows(1, 15, diagonals)
+    over_rows(4, 12, diagonals, strips=())
 
     def divergence(row, ref, f):
         return (
@@ -459,9 +547,6 @@
         row.put(gv, 0, row.at(mat, 1) * divergence(row, xu, 1))
 
     over_rows(3, 12, old_scaled, strips=(L,))
-
-    for copy in loads[4:]:
-        copy.wait()
 
     def first(row):
         j = row.i - 4
@@ -487,13 +572,15 @@
 
     over_rows(4, 12, first, OWN, ())
 
-    exchange(
-        [
-            (z0, 1, 4, pk_z0, pl_z0, pr_z0, ys_z0, yr_z0),
-            (ze, 3, 2, pk_ze, pl_ze, pr_ze, ys_ze, yr_ze),
-        ],
-        4,
-    )
+    round_2.pack()
+    round_2.start()
+    over_rows(0, 3, materials, strips=())
+    over_rows(13, 16, materials, strips=())
+    over_rows(0, 3, faces, strips=())
+    over_rows(12, 15, faces)
+    over_rows(1, 4, diagonals, strips=())
+    over_rows(12, 15, diagonals)
+    round_2.finish()
 
     def second(row):
         center = row.at(z0, 0)
@@ -580,9 +667,9 @@
             new[k] = new[k] + heft * div[p] * div[q]
         return tuple(a + fold(b) for a, b in zip(sums, new))
 
-    sums = lax.fori_loop(4, 12, pressure_moments, (zero,) * 4)
-    sums += lax.fori_loop(4, 12, plain_moments, (zero,) * 18)
-    sums += lax.fori_loop(4, 12, energy_moments, (zero,) * 6)
+    sums = lax.fori_loop(4, 12, pressure_moments, (zero,) * 4, unroll=4)
+    sums += lax.fori_loop(4, 12, plain_moments, (zero,) * 18, unroll=4)
+    sums += lax.fori_loop(4, 12, energy_moments, (zero,) * 6, unroll=4)
     for k, value in enumerate(sums):
         rows[k : k + 1, :] = jnp.sum(value, axis=0, keepdims=True)
     eye = lax.broadcasted_iota(jnp.int32, (32, 128), 0) == lax.broadcasted_iota(
@@ -592,12 +679,20 @@
     part[0] = jnp.sum(jnp.where(eye, column, 0.0), axis=0, keepdims=True)
 
     slot = 0
-    for stage, (group, got) in enumerate(((group_a, got_a), (group_b, got_b), (group_c, got_c))):
-        if stage == 2 and ny > 2 * reach + 1:
+    for stage, (group, got) in enumerate(((group_a, got_a), (group_b, got_b))):
+        if stage == 1 and chained:
             pl.semaphore_wait(known, 2)
-        copies = []
-        for k, device in enumerate(group):
-            copies.append(send(part.at[stage], got.at[k], (rs_sem, rr_sem), slot + k, device))
+        copies = [
+            pltpu.make_async_remote_copy(
+                src_ref=part.at[stage],
+                dst_ref=got.at[k],
+                send_sem=rs_sem.at[slot + k],
+                recv_sem=rr_sem.at[slot + k],
+                device_id=other,
+                device_id_type=MESH,
+            )
+            for k, other in enumerate(group)
+        ]
         slot += len(group)
         for copy in copies:
             copy.start()
@@ -608,7 +703,7 @@
             total = total + got[k]
         part[stage + 1] = total
 
-    column = jnp.sum(jnp.where(eye, part[3], 0.0), axis=1, keepdims=True)
+    column = jnp.sum(jnp.where(eye, part[2], 0.0), axis=1, keepdims=True)
     m = [column[k : k + 1, :] for k in range(28)]
 
     def steps(m0, m1, m2, m3):
@@ -658,13 +753,25 @@
     def vmem(*shape):
         return pltpu.VMEM(shape, F32)
 
-    moving = ((2, 4), (4, 1), (1, 4), (3, 2))
-    packs = [vmem(n, 16, 128) for n, _ in moving]
-    y_parts = [vmem(2, n, 10 + 2 * d, d, 128) for n, d in moving]
-    group_a, group_b, group_c = (cores * xs, (nx // cores) * (nz // xs), ny)
-    sent = group_a + group_b + group_c - 3
+    def strips(n):
+        g = -(-n // 4)
+        return (
+            vmem(n, 16, 128),
+            vmem(2, g, 16, 128),
+            vmem(2, n, 4, 128),
+            vmem(2, 2, g, 4, 128),
+            vmem(2, n, 16, 128),
+            vmem(2, 2, g, 16, 128),
+            vmem(2, 2, n, 4, 128),
+            vmem(2, 2, 2, g, 4, 128),
+        )
+
+    moving = ((4, 1), (2, 4), (1, 4), (3, 2))
+    count_a, count_b = (nx // cores * nz - 1, ny * cores - 1)
+    sent = max(count_a + count_b, 1)
     dma = pltpu.SemaphoreType.DMA
     scratch = [
+        *[pltpu.SMEM((ZONES,), F32) for _ in range(3)],
         vmem(8, 16, 128),
         vmem(8, 16, 128),
         vmem(3, 8, 16, 128),
@@ -683,24 +790,22 @@
         field(3),
         field(9),
         field(3),
-        *packs,
-        *packs,
-        *packs,
-        *y_parts,
-        *y_parts,
+        *[vmem(2, n, 8, d, 128) for n, d in moving],
+        *[vmem(2, n, 8 + 2 * d, d, 128) for n, d in moving],
+        strips(6),
+        strips(4),
         vmem(32, 128),
-        vmem(4, 1, 128),
-        vmem(max(group_a - 1, 1), 1, 128),
-        vmem(max(group_b - 1, 1), 1, 128),
-        vmem(max(group_c - 1, 1), 1, 128),
-        dma((7,)),
-        *[dma((8,)) for _ in range(6)],
-        dma((max(sent, 1),)),
-        dma((max(sent, 1),)),
+        vmem(3, 1, 128),
+        vmem(max(count_a, 1), 1, 128),
+        vmem(max(count_b, 1), 1, 128),
+        dma((10,)),
+        dma((68,)),
+        dma((68,)),
+        dma((sent,)),
+        dma((sent,)),
         pltpu.SemaphoreType.REGULAR,
     ]
-    anywhere = pl.BlockSpec(memory_space=pl.ANY)
-    scalars = pl.BlockSpec(memory_space=pltpu.SMEM)
+    far = pl.BlockSpec(memory_space=pltpu.HBM)
     near = pl.BlockSpec(memory_space=pltpu.VMEM)
     return pl.pallas_call(
         functools.partial(kernel, sizes),
@@ -710,11 +815,11 @@
             jax.ShapeDtypeStruct((3, 8, 16, 128), F32),
             jax.ShapeDtypeStruct((8, 16, 128), F32),
         ),
-        in_specs=[anywhere] * 7 + [scalars] * 3,
+        in_specs=[far] * 10,
         out_specs=(near, near, near),
         scratch_shapes=scratch,
         compiler_params=pltpu.CompilerParams(
-            collective_id=0, has_side_effects=True, vmem_limit_bytes=48 * 1024 * 1024
+            collective_id=0, has_side_effects=True, vmem_limit_bytes=67043328
         ),
     )(*args)
 

time: 89.8 us -> 67.5 us (0.75)
  Pallas kernels: 78.5 us -> 62.9 us
  local copies, waits for them, and re-layouts: 9.94 us -> 3.75 us
    pallas_call x1, Pallas kernels: 78.5 us -> 62.9 us  [local_step(): pl.pallas_call(functools.partial(kernel, sizes), name='biot_step', out_sh...]
    unnamed x23 -> x5, local copies, waits for them, and re-layouts: 9.94 us -> 3.75 us
where the time goes in v2:
time: 67.5 us; the launch traced here: 67.3 us
  Pallas kernels  62.9 us (93%)
  local copies, waits for them, and re-layouts  3.75 us (6%)
    pallas_call x1, Pallas kernels, local_step(): pl.pallas_call(functools.partial(kernel, sizes), name='biot_step', out_sh...  62.9 us
    unnamed x5, local copies, waits for them, and re-layouts  3.75 us

profile of v2, /device:TPU:1, one launch (start us, length us, event | category | flops | bytes accessed | tf_op | source)
XLA Modules:
  0.0 67.3 jit_solution(11864007339940254710)
XLA Ops:
  0.6 62.9 %biot_step.1 = (f32[8,16,128]{2,1,0:T(8,128)}, f32[3,8,16,128]{3,2,1,0:T(8,128)}, f32[8,16,128]{2,1,0:T(8,128)}) custom-call(f32[8,16,128]{2,1,0:T(8,128)} %source.1, f32[8,16,128]{2,1,0:T(8,128)} %press_old.1, f32[8,16,128]{2,1,0:T(8,128)} %strain_prev.1, f32[3,8,16,128]{3,2,1,0:T(8,128)} %motion_old.1, f32[3,8,16,128]{3,2,1,0:T(8,128)} %body_force.1, ...), custom_call_target="tpu_custom_call" | custom-call | tf_op jit(solution)/shard_map/biot_step/pallas_call | solution.py:810
  63.5 1.5 %copy.16 = f32[8,16,128]{2,1,0:T(8,128)} copy(f32[8,16,128]{2,1,0:T(8,128)} %get-tuple-element.6) | data formatting | bytes 131072
  65.0 0.0 copy-start
  65.0 1.6 %copy.17 = f32[3,8,16,128]{3,2,1,0:T(8,128)} copy(f32[3,8,16,128]{3,2,1,0:T(8,128)} %get-tuple-element.7) | data formatting | bytes 393216
  66.7 0.0 copy-done
  66.7 0.6 copy.18
Async XLA Ops:
  65.0 1.7 %copy-start = (f32[8,16,128]{2,1,0:T(8,128)S(1)}, f32[8,16,128]{2,1,0:T(8,128)}, u32[]{:S(2)}) copy-start(f32[8,16,128]{2,1,0:T(8,128)} %get-tuple-element.8) | copy-start | bytes 196612

commit v3 on v2

--- a/solution.py
+++ b/solution.py
@@ -118,7 +118,7 @@
     sp,
     gv,
     se,
-    mo,
+    cd,
     ys_xu,
     ys_zd,
     ys_z0,
@@ -173,12 +173,15 @@
 
     yh, core = (gx // cores, lax.rem(gx, cores))
     yl, xx = (gz // xs, lax.rem(gz, xs))
+
+    def far(step, count):
+        return -min(step % count, -step % count)
+
+    steps_a = [(h, k, x) for h in range(yhs) for k in range(yls) for x in range(xs) if h or k or x]
+    steps_a.sort(key=lambda t: far(t[0] * yls + t[1], yhs * yls) + far(t[2], xs))
     group_a = [
         (turn(yh, h, yhs) * cores + core, gy, turn(yl, k, yls) * xs + turn(xx, x, xs))
-        for h in range(yhs)
-        for k in range(yls)
-        for x in range(xs)
-        if h or k or x
+        for h, k, x in steps_a
     ]
     reach = 4
     chained = ny > 2 * reach + 1
@@ -186,7 +189,9 @@
     def over_z(k, c):
         return (yh * cores + turn(core, c, cores), turn(gy, k, ny), gz)
 
-    group_b = [over_z(k, c) for k in range(ny) for c in range(cores) if k or c]
+    steps_b = [(k, c) for k in range(ny) for c in range(cores) if k or c]
+    steps_b.sort(key=lambda t: far(t[0], ny))
+    group_b = [over_z(k, c) for k, c in steps_b]
     if chained:
         near = [
             over_z(k, c)
@@ -196,16 +201,6 @@
         ]
     else:
         near = group_b
-
-    barrier = pltpu.get_barrier_semaphore()
-    for way in ways:
-
-        @pl.when(there(way))
-        def _(way=way):
-            pl.semaphore_signal(barrier, inc=1, device_id=device(way), device_id_type=MESH)
-
-    for other in group_a + near:
-        pl.semaphore_signal(barrier, inc=1, device_id=other, device_id_type=MESH)
 
     loads = [
         pltpu.make_async_copy(src, dst, load_sem.at[k])
@@ -226,6 +221,16 @@
     ]
     for copy in loads:
         copy.start()
+
+    barrier = pltpu.get_barrier_semaphore()
+    for way in ways:
+
+        @pl.when(there(way))
+        def _(way=way):
+            pl.semaphore_signal(barrier, inc=1, device_id=device(way), device_id_type=MESH)
+
+    for other in group_a + near:
+        pl.semaphore_signal(barrier, inc=1, device_id=other, device_id_type=MESH)
 
     def send(src, dst, slot, to):
         return pltpu.make_async_remote_copy(
@@ -449,7 +454,7 @@
                 ref[f, i, 0:8, :] = jnp.zeros((8, 128), F32)
                 ref[f, i, 24:32, :] = jnp.zeros((8, 128), F32)
 
-    for ref in (zd, xu, z0, ze, mat, tf, mf, sp, gv, se, mo):
+    for ref in (zd, xu, z0, ze, mat, tf, mf, sp, gv, se):
         clear(ref)
     round_1.blank()
     round_2.blank()
@@ -678,7 +683,19 @@
     column = jnp.sum(rows[...], axis=1, keepdims=True)
     part[0] = jnp.sum(jnp.where(eye, column, 0.0), axis=0, keepdims=True)
 
+    def strains(row):
+        for k, (ref, f) in enumerate(
+            ((xu, 1), (ze, 0), (ze, 3), (ze, 6), (se, 0), (se, 3), (se, 6))
+        ):
+            cd[k, row.i - 4] = 0.5 * (
+                row.xp(ref, f)
+                - row.xm(ref, f)
+                + (row.yp(ref, f + 1) - row.ym(ref, f + 1))
+                + (row.zp(ref, f + 2) - row.zm(ref, f + 2))
+            )
+
     slot = 0
+    sent = []
     for stage, (group, got) in enumerate(((group_a, got_a), (group_b, got_b))):
         if stage == 1 and chained:
             pl.semaphore_wait(known, 2)
@@ -696,8 +713,11 @@
         slot += len(group)
         for copy in copies:
             copy.start()
+        sent += copies
+        if stage == 0:
+            over_rows(4, 12, strains, OWN, ())
         for copy in copies:
-            copy.wait()
+            copy.wait_recv()
         total = part[stage]
         for k in range(len(group)):
             total = total + got[k]
@@ -721,27 +741,39 @@
 
     ea, eb = steps(*[quadratic(m[4 + 6 * k : 10 + 6 * k]) for k in range(4)])
 
-    def moved(row):
-        for c in range(3):
-            z = row.at(ze, c) + a * row.at(ze, 3 + c) + b * row.at(ze, 6 + c)
-            s = row.at(se, c) + a * row.at(se, 3 + c) + b * row.at(se, 6 + c)
-            row.put(mo, c, row.at(xu, 1 + c) + ea * z + eb * s)
-
-    over_rows(3, 13, moved)
-
-    def finish(row):
-        j = row.i - 4
+    def finish(i, carry):
+        row = Row(i, OWN, False)
+        j = i - 4
         press_out[j] = row.at(xu, 0) + a * row.at(z0, 0) + b * row.at(sp, 0)
         for c in range(3):
-            motion_out[c, j] = row.at(mo, c)
-        strain_out[j] = 0.5 * (
-            row.xp(mo, 0)
-            - row.xm(mo, 0)
-            + (row.yp(mo, 1) - row.ym(mo, 1))
-            + (row.zp(mo, 2) - row.zm(mo, 2))
-        )
-
-    over_rows(4, 12, finish, OWN, ())
+            total = row.at(xu, 1 + c)
+            for p in range(3):
+                total = total + weights[p] * row.at(ze, 3 * p + c)
+                total = total + weights[3 + p] * row.at(se, 3 * p + c)
+            motion_out[c, j] = total
+        total = cd[0, j]
+        for k in range(6):
+            total = total + weights[k] * cd[1 + k, j]
+        strain_out[j] = total
+        return carry
+
+    weights = (ea, ea * a, ea * b, eb, eb * a, eb * b)
+    lax.fori_loop(4, 12, finish, 0, unroll=4)
+    for copy in sent:
+        copy.wait_send()
+
+
+def hand_over(*refs):
+    src, dst, held, (come, go) = (refs[0:3], refs[3:6], refs[6:9], refs[9:11])
+    incoming = [pltpu.make_async_copy(a, h, come.at[k]) for k, (a, h) in enumerate(zip(src, held))]
+    outgoing = [pltpu.make_async_copy(h, b, go.at[k]) for k, (h, b) in enumerate(zip(held, dst))]
+    for copy in incoming:
+        copy.start()
+    for copy, onward in zip(incoming, outgoing):
+        copy.wait()
+        onward.start()
+    for onward in outgoing:
+        onward.wait()
 
 
 def local_step(sizes, *args):
@@ -789,7 +821,7 @@
         field(1),
         field(3),
         field(9),
-        field(3),
+        vmem(7, 8, 16, 128),
         *[vmem(2, n, 8, d, 128) for n, d in moving],
         *[vmem(2, n, 8 + 2 * d, d, 128) for n, d in moving],
         strips(6),
@@ -807,7 +839,7 @@
     ]
     far = pl.BlockSpec(memory_space=pltpu.HBM)
     near = pl.BlockSpec(memory_space=pltpu.VMEM)
-    return pl.pallas_call(
+    done = pl.pallas_call(
         functools.partial(kernel, sizes),
         name="biot_step",
         out_shape=(
@@ -822,6 +854,17 @@
             collective_id=0, has_side_effects=True, vmem_limit_bytes=67043328
         ),
     )(*args)
+    shapes = [(8, 16, 128), (3, 8, 16, 128), (8, 16, 128)]
+    return tuple(
+        pl.pallas_call(
+            hand_over,
+            name="hand_over",
+            out_shape=tuple(jax.ShapeDtypeStruct(shape, F32) for shape in shapes),
+            in_specs=[far] * 3,
+            out_specs=(far, far, far),
+            scratch_shapes=[*[vmem(*shape) for shape in shapes], dma((3,)), dma((3,))],
+        )(*done)
+    )
 
 
 def solution(mesh, cores=2, xs=4):

time: 67.5 us -> 65.3 us (0.967)
  local copies, waits for them, and re-layouts: 3.75 us -> 0 us
  Pallas kernels: 62.9 us -> 64.4 us
    unnamed x5 -> x0, local copies, waits for them, and re-layouts: 3.75 us -> none
    pallas_call x0 -> x1, Pallas kernels: none -> 1.71 us  [local_step(): pl.pallas_call(hand_over, name='hand_over', out_shape=tuple((jax.ShapeDty...]
where the time goes in v3:
time: 65.3 us; the launch traced here: 65.1 us
  Pallas kernels  64.4 us (99%)
    pallas_call x1, Pallas kernels, local_step(): pl.pallas_call(functools.partial(kernel, sizes), name='biot_step', out_sh...  62.7 us
    pallas_call x1, Pallas kernels, local_step(): pl.pallas_call(hand_over, name='hand_over', out_shape=tuple((jax.ShapeDty...  1.71 us

profile of v3, /device:TPU:1, one launch (start us, length us, event | category | flops | bytes accessed | tf_op | source)
XLA Modules:
  0.0 65.1 jit_solution(187428178492569265)
XLA Ops:
  0.6 62.7 %biot_step.1 = (f32[8,16,128]{2,1,0:T(8,128)}, f32[3,8,16,128]{3,2,1,0:T(8,128)}, f32[8,16,128]{2,1,0:T(8,128)}) custom-call(f32[8,16,128]{2,1,0:T(8,128)} %source.1, f32[8,16,128]{2,1,0:T(8,128)} %press_old.1, f32[8,16,128]{2,1,0:T(8,128)} %strain_prev.1, f32[3,8,16,128]{3,2,1,0:T(8,128)} %motion_old.1, f32[3,8,16,128]{3,2,1,0:T(8,128)} %body_force.1, ...), custom_call_target="tpu_custom_call" | custom-call | tf_op jit(solution)/shard_map/biot_step/pallas_call | solution.py:842
  63.4 1.7 %hand_over.1 = (f32[8,16,128]{2,1,0:T(8,128)}, f32[3,8,16,128]{3,2,1,0:T(8,128)}, f32[8,16,128]{2,1,0:T(8,128)}) custom-call(f32[8,16,128]{2,1,0:T(8,128)} %get-tuple-element.6.refs_0_, f32[3,8,16,128]{3,2,1,0:T(8,128)} %get-tuple-element.7.refs_1_, f32[8,16,128]{2,1,0:T(8,128)} %get-tuple-element.8.refs_2_), custom_call_target="tpu_custom_call" | custom-call | tf_op jit(solution)/shard_map/hand_over/pallas_call | solution.py:859
